TPU v7x, 256 devices: a whole 4x4x8 slice. The times are simulated.
256 devices in a mesh: query: 8 (over y, z_hi), ctx: 32 (over x, z_lo, core).
Axes of the slice: x: 4, y: 4, z: 8 (z_hi: 2, z_lo: 4; z = z_hi * 4 + z_lo), core: 2. Of those that a mesh axis runs over, the one named last changes fastest.
Arguments:
- query_states: bfloat16 [256, 3072], P('query'), may hold values from -370 to 370
- key_states: bfloat16 [32768, 3072], P('ctx', 'query'), may hold values from -10.5 to 10.5
- value_states: bfloat16 [32768, 3072], P('ctx', 'query'), may hold values from -6 to 6
- level_ids: int32 [32768], P('ctx'), may hold values from 0 to 4, as said below
- level_bias: float32 [5, 24], replicated, may hold values from -1.5 to 1.5
- live_counts: int32 [32], P('ctx'), may hold values from 256 to 1024, as said below
- out_grad: bfloat16 [256, 3072], P('query'), may hold values from -6 to 6
Outputs:
- attn_out: bfloat16 [256, 3072], P(('query', 'ctx'))
- query_grad: bfloat16 [256, 3072], P(('query', 'ctx'))
- key_grad: bfloat16 [32768, 3072], P('ctx', 'query')
- value_grad: bfloat16 [32768, 3072], P('ctx', 'query')
Inputs may be any that keep to these rules, and one draw needn't show every extreme that they name: Owner c's slots c * 1024 to c * 1024 + live_counts[c] - 1 are live, its other slots are empty; at least one owner has all 1024 slots live. `level_ids`: constant over each aligned run of 16 slots.
All inputs are finite; a program needn't handle non-finite values.
Results may differ from a plain program's by a relative error of at most 0.012.
Values may be sent and summed in bfloat16 or wider, within the bound.
A program may use at most 64 MiB of HBM per device.

v0:
```python
import math

import jax
import jax.numpy as jnp
from jax import lax
from jax.sharding import PartitionSpec as P


def copy_for_each(x, axis):
    copies = jnp.broadcast_to(x, (lax.axis_size(axis), *x.shape))
    return lax.all_to_all(copies, axis, split_axis=0, concat_axis=0, tiled=True)


def over_copies(x, axis):
    return copy_for_each(x, axis).max(axis=0)


def split_up(x, dim, peers):
    dims = x.shape
    pieces = x.reshape(*dims[:dim], peers, dims[dim] // peers, *dims[dim + 1 :])
    return jnp.moveaxis(pieces, dim, 0)


def sum_at_owner(x, axis, dim):
    peers = lax.axis_size(axis)
    pieces = lax.all_to_all(split_up(x, dim, peers), axis, 0, 0, tiled=True)
    return jnp.sum(pieces, axis=0)


def gather_turned(arrays, axis, dims):
    turned = [jnp.moveaxis(a, dim, 0) for a, dim in zip(arrays, dims)]
    widths = [t[0].size for t in turned]
    both = jnp.concatenate([t.reshape(-1, w) for t, w in zip(turned, widths)], axis=1)
    out = lax.all_gather(both, axis, axis=0, tiled=True)
    pieces = jnp.split(out, [sum(widths[:k]) for k in range(1, len(widths))], axis=1)
    return tuple(
        (
            jnp.moveaxis(b.reshape(-1, *t.shape[1:]), 0, dim)
            for b, t, dim in zip(pieces, turned, dims)
        )
    )


def rescale(outputs, factor):
    row_count = outputs.shape[0]
    head_count = factor.shape[0]
    return (outputs.reshape(row_count, head_count, -1) * factor.T[:, :, None]).reshape(
        row_count, -1
    )


def local(query_states, key_states, value_states, level_ids, level_bias, live_counts, out_grad):
    query_ways = lax.axis_size("query")
    owner_ways = lax.axis_size("ctx")
    level_count, head_total = level_bias.shape
    moved_queries, moved_grads = (
        lax.all_to_all(query_states, "query", split_axis=1, concat_axis=0, tiled=True),
        lax.all_to_all(out_grad, "query", split_axis=1, concat_axis=0, tiled=True),
    )
    rows_total = moved_queries.shape[0]
    part_rows = rows_total // query_ways // owner_ways

    def regroup(array):
        return jnp.transpose(
            array.reshape(query_ways, owner_ways, part_rows, -1), (1, 0, 2, 3)
        ).reshape(rows_total, -1)

    queries_in = regroup(moved_queries)
    grads_in = regroup(moved_grads)
    key_full, value_full = (key_states, value_states)
    head_count = head_total // query_ways
    bias_table = lax.dynamic_slice_in_dim(
        level_bias, lax.axis_index("query") * head_count, head_count, 1
    )
    query_count, feature_count = queries_in.shape
    slot_count = key_full.shape[0]
    head_size = feature_count // head_count
    softmax_scale = 1.0 / math.sqrt(head_size)
    queries = queries_in.reshape(query_count, head_count, head_size)
    key_heads = key_full.reshape(slot_count, head_count, head_size)
    value_heads = value_full.reshape(slot_count, head_count, head_size)
    grad_heads = grads_in.reshape(query_count, head_count, head_size)
    live_slots = lax.broadcasted_iota(jnp.int32, (slot_count,), 0) < live_counts[0]
    level_onehot = (
        level_ids[:, None] == lax.broadcasted_iota(jnp.int32, (1, level_count), 1)
    ).astype(jnp.float32)
    level_term = jnp.dot(
        level_onehot,
        bias_table,
        precision=lax.Precision.HIGHEST,
        preferred_element_type=jnp.float32,
    )
    scores = (
        jnp.einsum("qhd,khd->hqk", queries, key_heads, preferred_element_type=jnp.float32)
        * softmax_scale
    )
    scores = jnp.where(live_slots[None, None, :], scores + level_term.T[:, None, :], -1e30)
    local_max = jnp.max(scores, axis=2)
    raw_weights = jnp.exp(scores - local_max[..., None])
    local_sum = jnp.sum(raw_weights, axis=2)
    partial_value = jnp.einsum(
        "hqk,khd->qhd",
        raw_weights.astype(jnp.bfloat16),
        value_heads,
        preferred_element_type=jnp.float32,
    ).reshape(query_count, feature_count)
    row_count = query_count // owner_ways
    row_start = lax.axis_index("ctx") * row_count
    row_peak = over_copies(local_max, "ctx")
    factor = jnp.exp(local_max - row_peak)
    out_rows, sum_rows = (
        sum_at_owner(rescale(partial_value, factor), "ctx", 0),
        sum_at_owner(local_sum * factor, "ctx", 1),
    )
    peak_rows = lax.dynamic_slice_in_dim(row_peak, row_start, row_count, 1)
    attention_rows = out_rows.reshape(row_count, head_count, head_size) / sum_rows.T[:, :, None]
    grad_rows = lax.dynamic_slice_in_dim(grad_heads, row_start, row_count, 0)
    delta_rows = jnp.sum(grad_rows * attention_rows, axis=2).T
    log_rows = peak_rows + jnp.log(sum_rows)
    log_total, deltas = gather_turned((log_rows, delta_rows), "ctx", (1, 1))
    attn_rows = attention_rows.reshape(row_count, feature_count).astype(jnp.bfloat16)
    probabilities = jnp.exp(scores - log_total[..., None])
    dprobs = jnp.einsum("qhd,khd->hqk", grad_heads, value_heads, preferred_element_type=jnp.float32)
    dscores = (probabilities * (dprobs - deltas[..., None])).astype(jnp.bfloat16)
    prob_rounded = probabilities.astype(jnp.bfloat16)
    query_part = softmax_scale * jnp.einsum(
        "hqk,khd->qhd", dscores, key_heads, preferred_element_type=jnp.float32
    ).reshape(query_count, feature_count)
    query_rows = sum_at_owner(query_part, "ctx", 0).astype(jnp.bfloat16)
    block_shape = (head_count, owner_ways, query_ways, part_rows, slot_count)
    row_shape = (owner_ways, query_ways, part_rows, head_count, head_size)
    key_blocks = softmax_scale * jnp.einsum(
        "hcbrk,cbrhd->bkhd",
        dscores.reshape(block_shape),
        queries.reshape(row_shape),
        preferred_element_type=jnp.float32,
    )
    value_blocks = jnp.einsum(
        "hcbrk,cbrhd->bkhd",
        prob_rounded.reshape(block_shape),
        grad_heads.reshape(row_shape),
        preferred_element_type=jnp.float32,
    )
    key_cols = jnp.sum(key_blocks.astype(jnp.bfloat16).astype(jnp.float32), axis=0).reshape(
        slot_count, feature_count
    )
    value_cols = jnp.sum(value_blocks.astype(jnp.bfloat16).astype(jnp.float32), axis=0).reshape(
        slot_count, feature_count
    )
    attn_final, query_final = (
        lax.all_to_all(attn_rows, "query", split_axis=0, concat_axis=1, tiled=True),
        lax.all_to_all(query_rows, "query", split_axis=0, concat_axis=1, tiled=True),
    )
    return (attn_final, query_final, key_cols.astype(jnp.bfloat16), value_cols.astype(jnp.bfloat16))


def solution(mesh):
    placed = (
        P("query", None),
        P("ctx", "query"),
        P("ctx", "query"),
        P("ctx"),
        P(),
        P("ctx"),
        P("query", None),
    )
    return jax.shard_map(
        local,
        mesh=mesh,
        in_specs=placed,
        out_specs=(
            P(("query", "ctx"), None),
            P(("query", "ctx"), None),
            P("ctx", "query"),
            P("ctx", "query"),
        ),
        check_vma=False,
    )
```

profile of v0, /device:TPU:1, one launch (start us, length us, event | category | flops | bytes accessed | tf_op | source)
XLA Modules:
  0.0 183.3 jit_solution(12638040741019976941)
XLA Ops:
  2.3 11.6 %all-to-all-start = ((bf16[32,8,384]{2,0,1:T(8,128)(2,1)}), bf16[32,8,384]{2,0,1:T(8,128)(2,1)S(1)}, u32[]{:S(2)}, u32[]{:S(2)}) async-start(bf16[32,8,384]{2,0,1:T(8,128)(2,1)} %bitcast.82), calls=%async_computation | async-start | bytes 393216 | tf_op jit(solution)/shard_map/all_to_all | solution.py:57
  13.9 2.3 %copy.174 = bf16[1024,384]{0,1:T(8,128)(2,1)} copy(bf16[1024,384]{1,0:T(8,128)(2,1)} %param.8) | data formatting | bytes 1572864 | tf_op args[1]
  18.1 5.7 %all-to-all-done = bf16[32,8,384]{2,0,1:T(8,128)(2,1)S(1)} async-done(((bf16[32,8,384]{2,0,1:T(8,128)(2,1)}), bf16[32,8,384]{2,0,1:T(8,128)(2,1)S(1)}, u32[]{:S(2)}, u32[]{:S(2)}) %all-to-all-start) | async-done | bytes 196640 | tf_op jit(solution)/shard_map/all_to_all | solution.py:57
  24.5 1.9 %fusion.29 = (f32[3,256]{1,0:T(4,128)S(1)}, f32[3,256,1024]{2,1,0:T(8,128)S(1)}) fusion(f32[3,1024]{1,0:T(4,128)S(1)} %fusion.17, bf16[1024,3,128]{0,2,1:T(8,128)(2,1)} %bitcast.91, bf16[256,3,128]{2,1,0:T(4,128)(2,1)S(1)} %reshape_reshape.9, pred[1024]{0:T(1024)(128)(4,1)S(1)} %iota_compare_fusion.2), kind=kOutput, calls=%fused_computation.47 | convolution fusion | flops 204471552 | bytes 4145152 | tf_op jit(solution)/shard_map/qhd,khd->hqk/dot_general | solution.py:94
  27.0 9.1 %all-to-all-start.1 = ((f32[32,3,256]{2,1,0:T(4,128)}), f32[32,3,256]{2,1,0:T(4,128)S(1)}, u32[]{:S(2)}, u32[]{:S(2)}) async-start(f32[32,3,256]{2,1,0:T(4,128)} %broadcast_in_dim.16), calls=%async_computation.1 | async-start | bytes 262144 | tf_op jit(solution)/shard_map/all_to_all | solution.py:11
  36.1 2.3 %copy.177 = bf16[1024,384]{0,1:T(8,128)(2,1)} copy(bf16[1024,384]{1,0:T(8,128)(2,1)} %param.9) | data formatting | bytes 1572864 | tf_op args[2]
  40.0 4.8 %all-to-all-done.1 = f32[32,3,256]{2,1,0:T(4,128)S(1)} async-done(((f32[32,3,256]{2,1,0:T(4,128)}), f32[32,3,256]{2,1,0:T(4,128)S(1)}, u32[]{:S(2)}, u32[]{:S(2)}) %all-to-all-start.1) | async-done | bytes 98336 | tf_op jit(solution)/shard_map/all_to_all | solution.py:11
  44.8 3.4 %all-to-all-start.5 = ((bf16[32,8,384]{2,0,1:T(8,128)(2,1)}), bf16[32,8,384]{2,0,1:T(8,128)(2,1)S(1)}, u32[]{:S(2)}, u32[]{:S(2)}) async-start(bf16[32,8,384]{2,0,1:T(8,128)(2,1)} %bitcast.81), calls=%async_computation.5 | async-start | bytes 393216 | tf_op jit(solution)/shard_map/all_to_all | solution.py:58
  49.9 8.3 %all-to-all-done.5 = bf16[32,8,384]{2,0,1:T(8,128)(2,1)S(1)} async-done(((bf16[32,8,384]{2,0,1:T(8,128)(2,1)}), bf16[32,8,384]{2,0,1:T(8,128)(2,1)S(1)}, u32[]{:S(2)}, u32[]{:S(2)}) %all-to-all-start.5) | async-done | bytes 196640 | tf_op jit(solution)/shard_map/all_to_all | solution.py:58
  58.2 6.1 %all-to-all-start.3 = ((f32[32,3,8]{2,1,0:T(4,128)}), f32[32,3,8]{2,1,0:T(4,128)S(1)}, u32[]{:S(2)}, u32[]{:S(2)}) async-start(f32[32,3,8]{2,1,0:T(4,128)} %copy.181), calls=%async_computation.3 | async-start | bytes 131072 | tf_op jit(solution)/shard_map/all_to_all | solution.py:26
  67.3 2.0 %reshape_reshape.10 = f32[32,8,384]{2,1,0:T(8,128)} reshape(f32[256,3,128]{2,1,0:T(4,128)} %copy.180) | data formatting | bytes 786432 | tf_op jit(solution)/shard_map/reshape;reshape | solution.py:20
  69.3 2.9 %all-to-all-done.3 = f32[32,3,8]{2,1,0:T(4,128)S(1)} async-done(((f32[32,3,8]{2,1,0:T(4,128)}), f32[32,3,8]{2,1,0:T(4,128)S(1)}, u32[]{:S(2)}, u32[]{:S(2)}) %all-to-all-start.3) | async-done | bytes 3104 | tf_op jit(solution)/shard_map/all_to_all | solution.py:26
  72.8 4.8 %all-to-all-start.2 = ((f32[32,8,384]{2,1,0:T(8,128)}), f32[32,8,384]{2,1,0:T(8,128)S(1)}, u32[]{:S(2)}, u32[]{:S(2)}) async-start(f32[32,8,384]{2,1,0:T(8,128)} %reshape_reshape.10), calls=%async_computation.2 | async-start | bytes 786432 | tf_op jit(solution)/shard_map/all_to_all | solution.py:26
  84.1 7.5 %all-to-all-done.2 = f32[32,8,384]{2,1,0:T(8,128)S(1)} async-done(((f32[32,8,384]{2,1,0:T(8,128)}), f32[32,8,384]{2,1,0:T(8,128)S(1)}, u32[]{:S(2)}, u32[]{:S(2)}) %all-to-all-start.2) | async-done | bytes 393248 | tf_op jit(solution)/shard_map/all_to_all | solution.py:26
  93.3 39.9 %all_gather.3 = f32[256,6]{1,0:T(8,128)S(1)} all-gather(f32[8,6]{1,0:T(8,128)S(1)} %copy.186), channel_id=1, replica_groups=mesh['query'=8,'ctx'=32] {'ctx'}, dimensions={0}, use_global_device_ids=true | all-gather | bytes 6336 | tf_op jit(solution)/shard_map/all_gather | solution.py:34
  133.4 2.1 %multiply_convert_fusion.1 = bf16[3,256,1024]{2,1,0:T(8,128)(2,1)S(1)} fusion(f32[3,256,1024]{2,1,0:T(8,128)S(1)} %get-tuple-element.41, bf16[256,3,128]{2,0,1:T(8,128)(2,1)} %copy.185, bf16[1024,3,128]{0,2,1:T(8,128)(2,1)} %bitcast.87, f32[3,256]{1,0:T(4,128)S(1)} %copy.190, f32[3,256]{1,0:T(4,128)S(1)} %copy.187), kind=kOutput, calls=%fused_computation.3 | convolution fusion | flops 204472320 | bytes 5707776 | tf_op jit(solution)/shard_map/qhd,khd->hqk/dot_general | solution.py:123
  138.4 2.0 %mul.66 = f32[32,8,384]{2,1,0:T(8,128)} reshape(f32[256,3,128]{2,1,0:T(4,128)} %copy.192) | data formatting | bytes 786432 | tf_op jit(solution)/shard_map/mul | solution.py:126
  140.4 3.8 %all-to-all-start.6 = ((f32[32,8,384]{2,1,0:T(8,128)}), f32[32,8,384]{2,1,0:T(8,128)S(1)}, u32[]{:S(2)}, u32[]{:S(2)}) async-start(f32[32,8,384]{2,1,0:T(8,128)} %mul.66), calls=%async_computation.6 | async-start | bytes 786432 | tf_op jit(solution)/shard_map/all_to_all | solution.py:26
  148.2 6.0 %fusion = bf16[3,1024,128]{2,1,0:T(8,128)(2,1)} fusion(bf16[3,32,8,1024]{3,2,1,0:T(8,128)(2,1)} %bitcast.88, bf16[32,8,3,128]{3,1,2,0:T(8,128)(2,1)} %bitcast.94), kind=kOutput, calls=%fused_computation.1 | convolution fusion | flops 210370560 | bytes 2555904 | tf_op jit(solution)/shard_map/hcbrk,cbrhd->bkhd/dot_general | solution.py:132
  154.2 4.0 %all-to-all-done.6 = f32[32,8,384]{2,1,0:T(8,128)S(1)} async-done(((f32[32,8,384]{2,1,0:T(8,128)}), f32[32,8,384]{2,1,0:T(8,128)S(1)}, u32[]{:S(2)}, u32[]{:S(2)}) %all-to-all-start.6) | async-done | bytes 393248 | tf_op jit(solution)/shard_map/all_to_all | solution.py:26
  158.2 3.3 %all-to-all-start.4 = ((bf16[8,2,192]{2,1,0:T(2,128)(2,1)}), bf16[8,2,192]{2,1,0:T(2,128)(2,1)S(1)}, u32[]{:S(2)}, u32[]{:S(2)}) async-start(bf16[8,2,192]{2,1,0:T(2,128)(2,1)} %reshape.124), calls=%async_computation.4 | async-start | bytes 16384 | tf_op jit(solution)/shard_map/all_to_all | solution.py:151
  164.7 5.8 %all-to-all-done.4 = bf16[8,2,192]{2,1,0:T(2,128)(2,1)S(1)} async-done(((bf16[8,2,192]{2,1,0:T(2,128)(2,1)}), bf16[8,2,192]{2,1,0:T(2,128)(2,1)S(1)}, u32[]{:S(2)}, u32[]{:S(2)}) %all-to-all-start.4) | async-done | bytes 6176 | tf_op jit(solution)/shard_map/all_to_all | solution.py:151
  170.5 3.3 %all-to-all-start.7 = ((bf16[8,2,192]{2,1,0:T(2,128)(2,1)}), bf16[8,2,192]{2,1,0:T(2,128)(2,1)S(1)}, u32[]{:S(2)}, u32[]{:S(2)}) async-start(bf16[8,2,192]{2,1,0:T(2,128)(2,1)} %reshape.126), calls=%async_computation.7 | async-start | bytes 16384 | tf_op jit(solution)/shard_map/all_to_all | solution.py:152
  173.8 4.2 %convert_reduce_fusion = bf16[3,1024,128]{2,1,0:T(8,128)(2,1)S(1)} fusion(bf16[3,32,8,1024]{3,2,1,0:T(8,128)(2,1)} %fusion.4, bf16[32,8,3,128]{3,1,2,0:T(8,128)(2,1)} %bitcast.96), kind=kOutput, calls=%fused_computation.2 | convolution fusion | flops 207224832 | bytes 2555904 | tf_op jit(solution)/shard_map/hcbrk,cbrhd->bkhd/dot_general | solution.py:138
  (63 shorter events, 34.6 us)
Async XLA Ops:
  0.6 16.2 %copy-start = (f32[5,24]{1,0:T(8,128)S(1)}, f32[5,24]{1,0:T(8,128)}, u32[]{:S(2)}) copy-start(f32[5,24]{1,0:T(8,128)} %param.11) | copy-start | bytes 1444
  2.3 21.5 %all-to-all-start = ((bf16[32,8,384]{2,0,1:T(8,128)(2,1)}), bf16[32,8,384]{2,0,1:T(8,128)(2,1)S(1)}, u32[]{:S(2)}, u32[]{:S(2)}) async-start(bf16[32,8,384]{2,0,1:T(8,128)(2,1)} %bitcast.82), calls=%async_computation | async-start | bytes 393216 | tf_op jit(solution)/shard_map/all_to_all | solution.py:57
  23.8 0.7 copy-start.3
  27.0 17.8 %all-to-all-start.1 = ((f32[32,3,256]{2,1,0:T(4,128)}), f32[32,3,256]{2,1,0:T(4,128)S(1)}, u32[]{:S(2)}, u32[]{:S(2)}) async-start(f32[32,3,256]{2,1,0:T(4,128)} %broadcast_in_dim.16), calls=%async_computation.1 | async-start | bytes 262144 | tf_op jit(solution)/shard_map/all_to_all | solution.py:11
  44.8 13.4 %all-to-all-start.5 = ((bf16[32,8,384]{2,0,1:T(8,128)(2,1)}), bf16[32,8,384]{2,0,1:T(8,128)(2,1)S(1)}, u32[]{:S(2)}, u32[]{:S(2)}) async-start(bf16[32,8,384]{2,0,1:T(8,128)(2,1)} %bitcast.81), calls=%async_computation.5 | async-start | bytes 393216 | tf_op jit(solution)/shard_map/all_to_all | solution.py:58
  58.2 11.0 %copy-start.5 = (bf16[32,8,384]{2,0,1:T(8,128)(2,1)}, bf16[32,8,384]{2,0,1:T(8,128)(2,1)S(1)}, u32[]{:S(2)}) copy-start(bf16[32,8,384]{2,0,1:T(8,128)(2,1)S(1)} %all-to-all-done.5) | copy-start | bytes 589828
  58.2 13.9 %all-to-all-start.3 = ((f32[32,3,8]{2,1,0:T(4,128)}), f32[32,3,8]{2,1,0:T(4,128)S(1)}, u32[]{:S(2)}, u32[]{:S(2)}) async-start(f32[32,3,8]{2,1,0:T(4,128)} %copy.181), calls=%async_computation.3 | async-start | bytes 131072 | tf_op jit(solution)/shard_map/all_to_all | solution.py:26
  72.2 0.6 copy-start.6
  72.8 18.8 %all-to-all-start.2 = ((f32[32,8,384]{2,1,0:T(8,128)}), f32[32,8,384]{2,1,0:T(8,128)S(1)}, u32[]{:S(2)}, u32[]{:S(2)}) async-start(f32[32,8,384]{2,1,0:T(8,128)} %reshape_reshape.10), calls=%async_computation.2 | async-start | bytes 786432 | tf_op jit(solution)/shard_map/all_to_all | solution.py:26
  83.5 0.7 copy-start.9
  133.4 3.9 %copy-start.7 = (f32[3,256]{1,0:T(4,128)}, f32[3,256]{1,0:T(4,128)S(1)}, u32[]{:S(2)}) copy-start(f32[3,256]{1,0:T(4,128)S(1)} %copy.187) | copy-start | bytes 9220
  133.4 3.3 %copy-start.2 = (bf16[1024,384]{0,1:T(8,128)(2,1)S(1)}, bf16[1024,384]{0,1:T(8,128)(2,1)}, u32[]{:S(2)}) copy-start(bf16[1024,384]{0,1:T(8,128)(2,1)} %copy.174) | copy-start | bytes 2359300
  135.6 1.2 copy-start.1
  140.4 17.8 %all-to-all-start.6 = ((f32[32,8,384]{2,1,0:T(8,128)}), f32[32,8,384]{2,1,0:T(8,128)S(1)}, u32[]{:S(2)}, u32[]{:S(2)}) async-start(f32[32,8,384]{2,1,0:T(8,128)} %mul.66), calls=%async_computation.6 | async-start | bytes 786432 | tf_op jit(solution)/shard_map/all_to_all | solution.py:26
  148.2 13.4 %copy-start.8 = (f32[3,256]{1,0:T(4,128)S(1)}, f32[3,256]{1,0:T(4,128)}, u32[]{:S(2)}) copy-start(f32[3,256]{1,0:T(4,128)} %copy-done.7) | copy-start | bytes 9220
  158.2 12.2 %all-to-all-start.4 = ((bf16[8,2,192]{2,1,0:T(2,128)(2,1)}), bf16[8,2,192]{2,1,0:T(2,128)(2,1)S(1)}, u32[]{:S(2)}, u32[]{:S(2)}) async-start(bf16[8,2,192]{2,1,0:T(2,128)(2,1)} %reshape.124), calls=%async_computation.4 | async-start | bytes 16384 | tf_op jit(solution)/shard_map/all_to_all | solution.py:151
  163.2 14.7 %copy-start.4 = (bf16[3,1024,128]{2,1,0:T(8,128)(2,1)S(1)}, bf16[3,1024,128]{2,1,0:T(8,128)(2,1)}, u32[]{:S(2)}) copy-start(bf16[3,1024,128]{2,1,0:T(8,128)(2,1)} %fusion) | copy-start | bytes 2359300
  170.5 12.2 %all-to-all-start.7 = ((bf16[8,2,192]{2,1,0:T(2,128)(2,1)}), bf16[8,2,192]{2,1,0:T(2,128)(2,1)S(1)}, u32[]{:S(2)}, u32[]{:S(2)}) async-start(bf16[8,2,192]{2,1,0:T(2,128)(2,1)} %reshape.126), calls=%async_computation.7 | async-start | bytes 16384 | tf_op jit(solution)/shard_map/all_to_all | solution.py:152
where the time goes:
time: 185 us; the launch traced here: 183 us
  starting transfers between devices  45.6 us (25%)
  waiting for transfers between devices  40 us (22%)
  blocking collectives  39.9 us (22%)
  local copies, waits for them, and re-layouts  29.4 us (16%)
  matrix products  17.8 us (10%)
  other arithmetic  9.17 us (5%)
    all_gather x1, blocking collectives, gather_turned(): out = lax.all_gather(both, axis, axis=0, tiled=True)  39.9 us
    all_to_all x3, starting transfers between devices, sum_at_owner(): pieces = lax.all_to_all(split_up(x, dim, peers), axis, 0, 0, tiled=True)  14.8 us
    all_to_all x3, waiting for transfers between devices, sum_at_owner(): pieces = lax.all_to_all(split_up(x, dim, peers), axis, 0, 0, tiled=True)  14.4 us
    unnamed x28, local copies, waits for them, and re-layouts  12 us
    all_to_all x1, starting transfers between devices, local(): lax.all_to_all(query_states, 'query', split_axis=1, concat_axis=0, tiled=...  11.6 us
    all_to_all x1, starting transfers between devices, copy_for_each(): return lax.all_to_all(copies, axis, split_axis=0, concat_axis=0, tiled=True)  9.11 us
    all_to_all x1, waiting for transfers between devices, local(): lax.all_to_all(out_grad, 'query', split_axis=1, concat_axis=0, tiled=True)  8.29 us
    dot_general x1, matrix products, local(): jnp.einsum('hcbrk,cbrhd->bkhd', dscores.reshape(block_shape), queries.res...  6.05 us
  transfers between devices with their start and end apart: 8, of which 8 were waited for; matrix products, arithmetic and copies ran while one was open for 23% of the time, Pallas kernels for 0%

commit v1 on v0

v1 whole, which is shorter than its diff:
```python
import math

import jax
import jax.numpy as jnp
from jax import lax
from jax.experimental import pallas as pl
from jax.experimental.pallas import tpu as pltpu
from jax.sharding import PartitionSpec as P

MESH = pl.DeviceIdType.MESH
F32 = jnp.float32
BF16 = jnp.bfloat16
HD = 128
HEADS = 3
COLS = HEADS * HD
ROWS = 256
SLOTS = 1024
CHUNK = 256
SCALE = 1.0 / math.sqrt(HD)
NT = (((1,), (1,)), ((), ()))
DEAD = -1e30


def dot_nt(a, b):
    return lax.dot_general(a, b, NT, preferred_element_type=F32)


def dot(a, b):
    return jnp.dot(a, b, preferred_element_type=F32)


def kernel(
    q_hbm, k_hbm, v_hbm, lid_hbm, lb_hbm, lc_hbm, g_hbm,
    attn_ref, dq_ref, kg_hbm, vg_hbm,
    own, gat, kv, kvt, bias, perm, w32, w16, dp, pb, dsb, ot, mx,
    sx, sz, sf, rx, fb, sy, ry, kvg, lid, lb, lc,
    ld, outsem, bsend, brecv, dsend, drecv, xsend, xrecv, zsend, zrecv,
    fsend, frecv, ysend, yrecv,
):
    q = lax.axis_index("query")
    c = lax.axis_index("ctx")
    y, zh = q // 2, q % 2
    x, zl, k = c // 8, (c // 2) % 4, c % 2
    g = x * 2 + k

    loads = [
        pltpu.make_async_copy(q_hbm, own.at[0], ld.at[0]),
        pltpu.make_async_copy(g_hbm, own.at[1], ld.at[1]),
        pltpu.make_async_copy(
            q_hbm.at[:, pl.ds(pl.multiple_of(q * COLS, HD), COLS)], gat.at[0, y], ld.at[2]
        ),
        pltpu.make_async_copy(
            g_hbm.at[:, pl.ds(pl.multiple_of(q * COLS, HD), COLS)], gat.at[1, y], ld.at[3]
        ),
        pltpu.make_async_copy(k_hbm, kv.at[0], ld.at[4]),
        pltpu.make_async_copy(v_hbm, kv.at[1], ld.at[5]),
        pltpu.make_async_copy(lid_hbm, lid, ld.at[6]),
        pltpu.make_async_copy(lb_hbm, lb, ld.at[7]),
        pltpu.make_async_copy(lc_hbm, lc, ld.at[8]),
    ]
    for copy in loads:
        copy.start()

    def ctx_of(xx, zz, kk):
        return xx * 8 + zz * 2 + kk

    def xk_peer(dg):
        gp = lax.rem(g + dg, 8)
        return gp, (q, ctx_of(gp // 2, zl, gp % 2))

    edge = zl % 3 == 0
    near, far = 3 - zl, 2 - zl // 3

    barrier = pltpu.get_barrier_semaphore()

    def greet(device):
        pl.semaphore_signal(barrier, inc=1, device_id=device, device_id_type=MESH)

    for dg in range(1, 8):
        greet(xk_peer(dg)[1])
    for d in range(1, 4):
        greet((lax.rem(y + d, 4) * 2 + zh, c))
        greet((q, ctx_of(x, lax.rem(zl + d, 4), k)))

    @pl.when(edge)
    def _():
        for d in range(4):
            greet((lax.rem(y + d, 4) * 2 + 1 - zh, ctx_of(x, near, k)))
            greet((lax.rem(y + d, 4) * 2 + 1 - zh, ctx_of(x, far, k)))
        pl.semaphore_wait(barrier, 21)

    @pl.when(jnp.logical_not(edge))
    def _():
        source = jnp.where(zl < 2, 3, 0)
        for d in range(4):
            greet((lax.rem(y + d, 4) * 2 + 1 - zh, ctx_of(x, source, k)))
        pl.semaphore_wait(barrier, 17)

    loads[0].wait()
    loads[1].wait()

    def block_send(yd, half, zz, slot, sem):
        qd = yd * 2 + half
        return pltpu.make_async_remote_copy(
            src_ref=own.at[k, :, pl.ds(pl.multiple_of(qd * COLS, HD), COLS)],
            dst_ref=gat.at[k, slot],
            send_sem=bsend.at[sem],
            recv_sem=brecv.at[slot],
            device_id=(qd, ctx_of(x, zz, k)),
            device_id_type=MESH,
        )

    sends = [block_send(lax.rem(y + d, 4), zh, zl, y, d) for d in (1, 3, 2)]
    cross = []
    for d in (2, 1, 3, 0):
        cross.append(block_send(lax.rem(y + d, 4), 1 - zh, far, 4 + y, 4 + d))
        cross.append(block_send(lax.rem(y + d, 4), 1 - zh, near, 4 + y, 8 + d))
    for copy in sends:
        copy.start()

    @pl.when(edge)
    def _():
        for copy in cross:
            copy.start()

    loads[6].wait()
    loads[7].wait()
    loads[8].wait()
    live = lc[0]

    def fill(t, carry):
        level = lid[t * 16]
        alive = lax.broadcasted_iota(jnp.int32, (16, HD), 0) + t * 16 < live
        for h in range(HEADS):
            bias[h, pl.ds(pl.multiple_of(t * 16, 16), 16), :] = jnp.where(
                alive, lb[level, q * HEADS + h], DEAD
            )
        return carry

    lax.fori_loop(0, SLOTS // 16, fill, 0)

    p_id = lax.broadcasted_iota(jnp.int32, (ROWS, ROWS), 0)
    i_id = lax.broadcasted_iota(jnp.int32, (ROWS, ROWS), 1)
    p_row = ((p_id >> 6) << 3) + (((p_id >> 3) & 3) << 1) + ((p_id >> 5) & 1)
    p_half = (p_id & 1) ^ zh
    place = (p_half << 7) + (((p_id >> 1) & 3) << 5) + p_row
    perm[...] = jnp.where(i_id == place, 1.0, 0.0).astype(BF16)
    fb[...] = jnp.zeros_like(fb)
    sx[pl.ds(g, 1)] = jnp.zeros((1, 8, ROWS), F32)

    loads[4].wait()
    loads[5].wait()
    for a in range(2):
        for h in range(HEADS):
            for t in range(SLOTS // CHUNK):
                rows = slice(t * CHUNK, (t + 1) * CHUNK)
                kvt[a, h * HD : (h + 1) * HD, rows] = kv[a, rows, h * HD : (h + 1) * HD].T
    loads[2].wait()
    loads[3].wait()

    partner = (q, ctx_of(x, zl, 1 - k))

    def pass_on(slot):
        return pltpu.make_async_remote_copy(
            src_ref=gat.at[k, slot],
            dst_ref=gat.at[k, slot],
            send_sem=dsend.at[slot],
            recv_sem=drecv.at[slot],
            device_id=partner,
            device_id_type=MESH,
        )

    def from_partner(slot):
        return pltpu.make_async_remote_copy(
            src_ref=gat.at[1 - k, slot],
            dst_ref=gat.at[1 - k, slot],
            send_sem=dsend.at[slot],
            recv_sem=drecv.at[slot],
            device_id=partner,
            device_id_type=MESH,
        )

    def arrived(slot):
        return pltpu.make_async_remote_copy(
            src_ref=gat.at[k, slot],
            dst_ref=gat.at[k, slot],
            send_sem=bsend.at[0],
            recv_sem=brecv.at[slot],
            device_id=partner,
            device_id_type=MESH,
        )

    def heads_of(a, h, lo, n):
        return gat[a, lo : lo + n, :, h * HD : (h + 1) * HD].reshape(n * 32, HD)

    def forward(half):
        lanes = slice(half * HD, (half + 1) * HD)
        for h in range(HEADS):
            cols = slice(h * HD, (h + 1) * HD)
            queries = heads_of(0, h, half * 4, 4)
            peak = jnp.full((1, HD), DEAD, F32)
            for t in range(SLOTS // CHUNK):
                rows = slice(t * CHUNK, (t + 1) * CHUNK)
                score = dot_nt(kv[0, rows, cols], queries) * SCALE + bias[h, rows, :]
                w32[h, rows, lanes] = score
                peak = jnp.maximum(peak, jnp.max(score, axis=0, keepdims=True))
            total = jnp.zeros((1, HD), F32)
            for t in range(SLOTS // CHUNK):
                rows = slice(t * CHUNK, (t + 1) * CHUNK)
                weight = jnp.exp(w32[h, rows, lanes] - peak)
                w32[h, rows, lanes] = weight
                w16[h, rows, lanes] = weight.astype(BF16)
                total = total + jnp.sum(weight, axis=0, keepdims=True)
            out = dot(kvt[1, cols, :], w16[h, :, lanes])
            ot[h, :, lanes] = out
            grads = heads_of(1, h, half * 4, 4).T.astype(F32)
            product = jnp.sum(out * grads, axis=0, keepdims=True)
            mx[h : h + 1, lanes] = peak
            sx[pl.ds(g, 1), h : h + 1, lanes] = (peak + jnp.log(total)).reshape(1, 1, HD)
            sx[pl.ds(g, 1), 4 + h : 5 + h, lanes] = (product / total).reshape(1, 1, HD)

    passed = []
    for half in range(2):
        slots = [lax.rem(y + d, 4) for d in (1, 3, 2)] if half == 0 else [4, 5, 6, 7]
        for slot in slots:
            arrived(slot).wait_recv()
            copy = pass_on(slot)
            copy.start()
            passed.append(copy)
        for slot in slots:
            from_partner(slot).wait_recv()
        forward(half)

    stat_sends = []
    for dg in range(1, 8):
        gp, device = xk_peer(dg)
        copy = pltpu.make_async_remote_copy(
            src_ref=sx.at[g], dst_ref=sx.at[g], send_sem=xsend.at[gp], recv_sem=xrecv.at[g],
            device_id=device, device_id_type=MESH,
        )
        copy.start()
        stat_sends.append(copy)

    for h in range(HEADS):
        for t in range(SLOTS // CHUNK):
            rows = slice(t * CHUNK, (t + 1) * CHUNK)
            dp[h, rows, :] = dot_nt(kv[1, rows, h * HD : (h + 1) * HD], heads_of(1, h, 0, 8))

    def merge(parts):
        logs, means = parts[:, 0:4, :], parts[:, 4:8, :]
        top = jnp.max(logs, axis=0)
        share = jnp.exp(logs - top[None])
        whole = jnp.sum(share, axis=0)
        return top + jnp.log(whole), jnp.sum(share * means, axis=0) / whole

    for dg in range(1, 8):
        gp, device = xk_peer(dg)
        pltpu.make_async_remote_copy(
            src_ref=sx.at[gp], dst_ref=sx.at[gp], send_sem=xsend.at[gp], recv_sem=xrecv.at[gp],
            device_id=device, device_id_type=MESH,
        ).wait_recv()
    logs, means = merge(sx[...])
    sz[pl.ds(zl, 1), 0:4, :] = logs[None]
    sz[pl.ds(zl, 1), 4:8, :] = means[None]
    for d in range(1, 4):
        zp = lax.rem(zl + d, 4)
        copy = pltpu.make_async_remote_copy(
            src_ref=sz.at[zl], dst_ref=sz.at[zl], send_sem=zsend.at[zp], recv_sem=zrecv.at[zl],
            device_id=(q, ctx_of(x, zp, k)), device_id_type=MESH,
        )
        copy.start()
        stat_sends.append(copy)
    for d in range(1, 4):
        zp = lax.rem(zl + d, 4)
        pltpu.make_async_remote_copy(
            src_ref=sz.at[zp], dst_ref=sz.at[zp], send_sem=zsend.at[zp], recv_sem=zrecv.at[zp],
            device_id=(q, ctx_of(x, zp, k)), device_id_type=MESH,
        ).wait_recv()
    log_total, deltas = merge(sz[...])

    factor = [jnp.exp(mx[h : h + 1, :] - log_total[h : h + 1, :]) for h in range(HEADS)]

    def to_owner_rows(a, h, turned):
        rows = dot_nt(perm[...], turned.astype(BF16)).astype(BF16)
        sf[a, :, :, h * HD : (h + 1) * HD] = rows.reshape(8, 32, HD)

    def send_rows(a):
        for dg in range(1, 8):
            gp, device = xk_peer(dg)
            copy = pltpu.make_async_remote_copy(
                src_ref=sf.at[a, gp], dst_ref=rx.at[a, g],
                send_sem=fsend.at[a, gp], recv_sem=frecv.at[a, g],
                device_id=device, device_id_type=MESH,
            )
            copy.start()
            stat_sends.append(copy)

    for h in range(HEADS):
        to_owner_rows(0, h, ot[h] * factor[h])
    send_rows(0)

    for h in range(HEADS):
        for t in range(SLOTS // HD):
            rows = slice(t * HD, (t + 1) * HD)
            prob = w32[h, rows, :] * factor[h]
            pb[h, rows, :] = prob.astype(BF16)
            dsb[h, rows, :] = (prob * (dp[h, rows, :] - deltas[h : h + 1, :])).astype(BF16)
        to_owner_rows(1, h, dot(kvt[0, h * HD : (h + 1) * HD, :], dsb[h]) * SCALE)
    send_rows(1)

    for h in range(HEADS):
        cols = slice(h * HD, (h + 1) * HD)
        for t in range(SLOTS // CHUNK):
            rows = slice(t * CHUNK, (t + 1) * CHUNK)
            kvg[0, rows, cols] = (dot(dsb[h, rows, :], heads_of(0, h, 0, 8)) * SCALE).astype(BF16)
            kvg[1, rows, cols] = dot(pb[h, rows, :], heads_of(1, h, 0, 8)).astype(BF16)
    outs = [
        pltpu.make_async_copy(kvg.at[0], kg_hbm, outsem.at[0]),
        pltpu.make_async_copy(kvg.at[1], vg_hbm, outsem.at[1]),
    ]
    for copy in outs:
        copy.start()

    for a in range(2):
        rx[a, pl.ds(g, 1)] = sf[a, pl.ds(g, 1)]
        for dg in range(1, 8):
            gp, device = xk_peer(dg)
            pltpu.make_async_remote_copy(
                src_ref=sf.at[a, gp], dst_ref=rx.at[a, gp],
                send_sem=fsend.at[a, gp], recv_sem=frecv.at[a, gp],
                device_id=device, device_id_type=MESH,
            ).wait_recv()
        summed = jnp.sum(rx[a].astype(F32), axis=0)
        for h in range(HEADS):
            fb[pl.ds(a * HEADS + h, 32, stride=8), :] = summed[:, h * HD : (h + 1) * HD]
    sy[...] = fb[...].astype(BF16).reshape(32, 8, HD)

    me = zl * 8 + q

    def row_copy(dz, dq, out):
        zp, qp = lax.rem(zl + dz, 4), lax.rem(q + dq, 8)
        d = zp * 8 + qp
        return pltpu.make_async_remote_copy(
            src_ref=sy.at[d], dst_ref=ry.at[me] if out else ry.at[d],
            send_sem=ysend.at[d], recv_sem=yrecv.at[me] if out else yrecv.at[d],
            device_id=(qp, ctx_of(x, zp, k)), device_id_type=MESH,
        )

    steps = [(dz, dq) for dz in range(4) for dq in range(8) if dz or dq]
    for dz, dq in steps:
        copy = row_copy(dz, dq, True)
        copy.start()
        stat_sends.append(copy)
    ry[pl.ds(me, 1)] = sy[pl.ds(me, 1)]
    for dz, dq in steps:
        row_copy(dz, dq, False).wait_recv()
    final = jnp.sum(ry[...].astype(F32).reshape(4, 8, 8, HD), axis=0)
    for qd in range(8):
        for h in range(HEADS):
            cols = slice((qd * HEADS + h) * HD, (qd * HEADS + h + 1) * HD)
            attn_ref[:, cols] = final[qd, h : h + 1, :].astype(BF16)
            dq_ref[:, cols] = final[qd, HEADS + h : HEADS + h + 1, :].astype(BF16)

    for copy in sends + passed + stat_sends:
        copy.wait_send()

    @pl.when(edge)
    def _():
        for copy in cross:
            copy.wait_send()

    for copy in outs:
        copy.wait()


def local(query_states, key_states, value_states, level_ids, level_bias, live_counts, out_grad):
    hbm = pl.BlockSpec(memory_space=pltpu.HBM)
    vmem = pl.BlockSpec(memory_space=pltpu.VMEM)
    dma = pltpu.SemaphoreType.DMA
    return pl.pallas_call(
        kernel,
        name="framepack",
        out_shape=(
            jax.ShapeDtypeStruct((1, 3072), BF16),
            jax.ShapeDtypeStruct((1, 3072), BF16),
            jax.ShapeDtypeStruct(key_states.shape, BF16),
            jax.ShapeDtypeStruct(value_states.shape, BF16),
        ),
        in_specs=[hbm] * 7,
        out_specs=(vmem, vmem, hbm, hbm),
        scratch_shapes=[
            pltpu.VMEM((2, 32, 3072), BF16),
            pltpu.VMEM((2, 8, 32, COLS), BF16),
            pltpu.VMEM((2, SLOTS, COLS), BF16),
            pltpu.VMEM((2, COLS, SLOTS), BF16),
            pltpu.VMEM((HEADS, SLOTS, HD), F32),
            pltpu.VMEM((ROWS, ROWS), BF16),
            pltpu.VMEM((HEADS, SLOTS, ROWS), F32),
            pltpu.VMEM((HEADS, SLOTS, ROWS), BF16),
            pltpu.VMEM((HEADS, SLOTS, ROWS), F32),
            pltpu.VMEM((HEADS, SLOTS, ROWS), BF16),
            pltpu.VMEM((HEADS, SLOTS, ROWS), BF16),
            pltpu.VMEM((HEADS, HD, ROWS), F32),
            pltpu.VMEM((8, ROWS), F32),
            pltpu.VMEM((8, 8, ROWS), F32),
            pltpu.VMEM((4, 8, ROWS), F32),
            pltpu.VMEM((2, 8, 32, COLS), BF16),
            pltpu.VMEM((2, 8, 32, COLS), BF16),
            pltpu.VMEM((ROWS, HD), F32),
            pltpu.VMEM((32, 8, HD), BF16),
            pltpu.VMEM((32, 8, HD), BF16),
            pltpu.VMEM((2, SLOTS, COLS), BF16),
            pltpu.SMEM((SLOTS,), jnp.int32),
            pltpu.SMEM((5, 24), F32),
            pltpu.SMEM((1,), jnp.int32),
            dma((9,)), dma((2,)),
            dma((12,)), dma((8,)),
            dma((8,)), dma((8,)),
            dma((8,)), dma((8,)),
            dma((4,)), dma((4,)),
            dma((2, 8)), dma((2, 8)),
            dma((32,)), dma((32,)),
        ],
        compiler_params=pltpu.CompilerParams(
            collective_id=0, has_side_effects=True, vmem_limit_bytes=56 * 1024 * 1024
        ),
    )(query_states, key_states, value_states, level_ids, level_bias, live_counts, out_grad)


def solution(mesh):
    placed = (
        P("query", None),
        P("ctx", "query"),
        P("ctx", "query"),
        P("ctx"),
        P(),
        P("ctx"),
        P("query", None),
    )
    return jax.shard_map(
        local,
        mesh=mesh,
        in_specs=placed,
        out_specs=(
            P(("query", "ctx"), None),
            P(("query", "ctx"), None),
            P("ctx", "query"),
            P("ctx", "query"),
        ),
        check_vma=False,
    )
```

time: 185 us -> 46.7 us (0.25)
  starting transfers between devices: 45.6 us -> 0 us
  Pallas kernels: 0 us -> 40.3 us
  waiting for transfers between devices: 40 us -> 0 us
  blocking collectives: 39.9 us -> 0 us
  local copies, waits for them, and re-layouts: 29.4 us -> 4.97 us
  matrix products: 17.8 us -> 0 us
  other arithmetic: 9.17 us -> 0 us
    all_to_all x8 -> x0, starting transfers between devices: 45.6 us -> none  [the longest x3 14.8 us: sum_at_owner(): pieces = lax.all_to_all(split_up(x, dim, peers), axis, 0, 0, tiled=True)]
    pallas_call x0 -> x1, Pallas kernels: none -> 40.3 us  [local(): pl.pallas_call(kernel, name='framepack', out_shape=(jax.ShapeDtypeStruct(...]
    all_to_all x8 -> x0, waiting for transfers between devices: 40 us -> none  [the longest x3 14.4 us: sum_at_owner(): pieces = lax.all_to_all(split_up(x, dim, peers), axis, 0, 0, tiled=True)]
    all_gather x1 -> x0, blocking collectives: 39.9 us -> none  [gather_turned(): out = lax.all_gather(both, axis, axis=0, tiled=True)]
    dot_general x7 -> x0, matrix products: 17.8 us -> none  [the longest x1 6.05 us: local(): jnp.einsum('hcbrk,cbrhd->bkhd', dscores.reshape(block_shape), queries.res...]
    unnamed x28 -> x8, local copies, waits for them, and re-layouts: 12 us -> 4.97 us
    another operation x4 -> x0, local copies, waits for them, and re-layouts: 5.4 us -> none  [the longest x2 3.34 us: local(): grad_heads = grads_in.reshape(query_count, head_count, head_size)]
    all_to_all x4 -> x0, local copies, waits for them, and re-layouts: 4.97 us -> none  [the longest x2 3.27 us: local(): lax.all_to_all(out_grad, 'query', split_axis=1, concat_axis=0, tiled=True)]
  transfers between devices with their start and end apart: 8 -> 0, of which waited for: 8 -> 0; matrix products, arithmetic and copies ran while one was open for 23% -> 0% of each run, Pallas kernels for 0% -> 0%
where the time goes in v1:
time: 46.7 us; the launch traced here: 46.5 us
  Pallas kernels  40.3 us (86%)
  local copies, waits for them, and re-layouts  4.97 us (11%)
  between operations  1.3 us (3%)
    pallas_call x1, Pallas kernels, local(): pl.pallas_call(kernel, name='framepack', out_shape=(jax.ShapeDtypeStruct(...  40.3 us
    unnamed x8, local copies, waits for them, and re-layouts  4.97 us

profile of v1, /device:TPU:1, one launch (start us, length us, event | category | flops | bytes accessed | tf_op | source)
XLA Modules:
  0.0 46.5 jit_solution(2720207649103729330)
XLA Ops:
  1.3 40.3 %framepack.1 = (bf16[1,3072]{1,0:T(2,128)(2,1)}, bf16[1,3072]{1,0:T(2,128)(2,1)}, bf16[1024,384]{1,0:T(8,128)(2,1)}, bf16[1024,384]{1,0:T(8,128)(2,1)}) custom-call(bf16[32,3072]{1,0:T(8,128)(2,1)} %q_hbm.1, bf16[1024,384]{1,0:T(8,128)(2,1)} %k_hbm.1, bf16[1024,384]{1,0:T(8,128)(2,1)} %v_hbm.1, s32[1024]{0:T(1024)} %lid_hbm.1, f32[5,24]{1,0:T(8,128)} %lb_hbm.1, ...), custom_call_target="tpu_custom_call" | custom-call | tf_op jit(solution)/shard_map/framepack/pallas_call | solution.py:380
  41.6 0.0 copy-start.1
  41.6 1.3 %copy.16 = bf16[1,3072]{1,0:T(2,128)(2,1)} copy(bf16[1,3072]{1,0:T(2,128)(2,1)} %get-tuple-element.8) | data formatting | bytes 12288
  42.9 0.0 copy-done.1
  42.9 0.6 %copy.17 = bf16[1,3072]{1,0:T(2,128)(2,1)} copy(bf16[1,3072]{1,0:T(2,128)(2,1)S(1)} %copy-done.1) | data formatting | bytes 12288
  43.5 0.0 copy-start
  43.5 2.2 %copy.18 = bf16[1024,384]{1,0:T(8,128)(2,1)} copy(bf16[1024,384]{1,0:T(8,128)(2,1)} %get-tuple-element.10) | data formatting | bytes 1572864
  45.7 0.0 copy-done
  45.7 0.9 %copy.19 = bf16[1024,384]{1,0:T(8,128)(2,1)} copy(bf16[1024,384]{1,0:T(8,128)(2,1)S(1)} %copy-done) | data formatting | bytes 1572864
Async XLA Ops:
  41.6 1.3 %copy-start.1 = (bf16[1,3072]{1,0:T(2,128)(2,1)S(1)}, bf16[1,3072]{1,0:T(2,128)(2,1)}, u32[]{:S(2)}) copy-start(bf16[1,3072]{1,0:T(2,128)(2,1)} %get-tuple-element.9) | copy-start | bytes 18436
  43.5 2.2 %copy-start = (bf16[1024,384]{1,0:T(8,128)(2,1)S(1)}, bf16[1024,384]{1,0:T(8,128)(2,1)}, u32[]{:S(2)}) copy-start(bf16[1024,384]{1,0:T(8,128)(2,1)} %get-tuple-element.11) | copy-start | bytes 2359300

commit v2 on v1

v2 whole, which is shorter than its diff:
```python
import math

import jax
import jax.numpy as jnp
from jax import lax
from jax.experimental import pallas as pl
from jax.experimental.pallas import tpu as pltpu
from jax.sharding import PartitionSpec as P

MESH = pl.DeviceIdType.MESH
F32 = jnp.float32
BF16 = jnp.bfloat16
HD = 128
HEADS = 3
COLS = HEADS * HD
ROWS = 256
SLOTS = 1024
CHUNK = 256
SCALE = 1.0 / math.sqrt(HD)
NT = (((1,), (1,)), ((), ()))
DEAD = -1e30


def dot_nt(a, b):
    return lax.dot_general(a, b, NT, preferred_element_type=F32)


def dot(a, b):
    return jnp.dot(a, b, preferred_element_type=F32)


def kernel(
    q_hbm, k_hbm, v_hbm, lid_hbm, lb_hbm, lc_hbm, g_hbm,
    attn_ref, dq_ref, kg_ref, vg_ref,
    own, gat, kv, kvt, bias, perm, w32, w16, dp, pb, dsb, mx,
    sx, sz, sf, rx, fb, sy, ry, lid, lb, lc,
    ld, bsend, brecv, dsend, drecv, xsend, xrecv, zsend, zrecv,
    fsend, frecv, ysend, yrecv,
):
    q = lax.axis_index("query")
    c = lax.axis_index("ctx")
    y, zh = q // 2, q % 2
    x, zl, k = c // 8, (c // 2) % 4, c % 2
    g = x * 2 + k

    loads = [
        pltpu.make_async_copy(q_hbm, own.at[0], ld.at[0]),
        pltpu.make_async_copy(g_hbm, own.at[1], ld.at[1]),
        pltpu.make_async_copy(
            q_hbm.at[:, pl.ds(pl.multiple_of(q * COLS, HD), COLS)], gat.at[0, y], ld.at[2]
        ),
        pltpu.make_async_copy(
            g_hbm.at[:, pl.ds(pl.multiple_of(q * COLS, HD), COLS)], gat.at[1, y], ld.at[3]
        ),
        pltpu.make_async_copy(k_hbm, kv.at[0], ld.at[4]),
        pltpu.make_async_copy(v_hbm, kv.at[1], ld.at[5]),
        pltpu.make_async_copy(lid_hbm, lid, ld.at[6]),
        pltpu.make_async_copy(lb_hbm, lb, ld.at[7]),
        pltpu.make_async_copy(lc_hbm, lc, ld.at[8]),
    ]
    for copy in loads:
        copy.start()

    def ctx_of(xx, zz, kk):
        return xx * 8 + zz * 2 + kk

    def xk_peer(dg):
        gp = lax.rem(g + dg, 8)
        return gp, (q, ctx_of(gp // 2, zl, gp % 2))

    edge = zl % 3 == 0
    near, far = 3 - zl, 2 - zl // 3

    barrier = pltpu.get_barrier_semaphore()

    def greet(device):
        pl.semaphore_signal(barrier, inc=1, device_id=device, device_id_type=MESH)

    for dg in range(1, 8):
        greet(xk_peer(dg)[1])
    for d in range(1, 4):
        greet((lax.rem(y + d, 4) * 2 + zh, c))
        greet((q, ctx_of(x, lax.rem(zl + d, 4), k)))

    @pl.when(edge)
    def _():
        for d in range(4):
            greet((lax.rem(y + d, 4) * 2 + 1 - zh, ctx_of(x, near, k)))
            greet((lax.rem(y + d, 4) * 2 + 1 - zh, ctx_of(x, far, k)))
        pl.semaphore_wait(barrier, 21)

    @pl.when(jnp.logical_not(edge))
    def _():
        source = jnp.where(zl < 2, 3, 0)
        for d in range(4):
            greet((lax.rem(y + d, 4) * 2 + 1 - zh, ctx_of(x, source, k)))
        pl.semaphore_wait(barrier, 17)

    loads[0].wait()
    loads[1].wait()

    def block_send(yd, half, zz, slot, sem):
        qd = yd * 2 + half
        return pltpu.make_async_remote_copy(
            src_ref=own.at[k, :, pl.ds(pl.multiple_of(qd * COLS, HD), COLS)],
            dst_ref=gat.at[k, slot],
            send_sem=bsend.at[sem],
            recv_sem=brecv.at[slot],
            device_id=(qd, ctx_of(x, zz, k)),
            device_id_type=MESH,
        )

    sends = [block_send(lax.rem(y + d, 4), zh, zl, y, d) for d in (1, 3, 2)]
    cross = []
    for d in (2, 1, 3, 0):
        cross.append(block_send(lax.rem(y + d, 4), 1 - zh, far, 4 + y, 4 + d))
        cross.append(block_send(lax.rem(y + d, 4), 1 - zh, near, 4 + y, 8 + d))
    for copy in sends:
        copy.start()

    @pl.when(edge)
    def _():
        for copy in cross:
            copy.start()

    loads[6].wait()
    loads[7].wait()
    loads[8].wait()
    live = lc[0]

    def fill(t, carry):
        level = lid[t * 16]
        alive = lax.broadcasted_iota(jnp.int32, (16, HD), 0) + t * 16 < live
        for h in range(HEADS):
            bias[h, pl.ds(pl.multiple_of(t * 16, 16), 16), :] = jnp.where(
                alive, lb[level, q * HEADS + h], DEAD
            )
        return carry

    lax.fori_loop(0, SLOTS // 16, fill, 0)

    p_id = lax.broadcasted_iota(jnp.int32, (HD, HD), 0)
    i_id = lax.broadcasted_iota(jnp.int32, (HD, HD), 1)
    p_row = ((p_id >> 5) << 3) + (((p_id >> 2) & 3) << 1) + ((p_id >> 4) & 1)
    perm[...] = jnp.where(i_id == ((p_id & 3) << 5) + p_row, 1.0, 0.0).astype(F32)
    own_rows = lax.broadcasted_iota(jnp.int32, (16, HD), 0)
    own_lane = ((own_rows & 3) << 5) + x * 8 + ((own_rows >> 2) << 1) + k
    pick = jnp.where(lax.broadcasted_iota(jnp.int32, (16, HD), 1) == own_lane, 1.0, 0.0)
    fb[...] = jnp.zeros_like(fb)
    for half in range(2):
        sx[half, pl.ds(g, 1)] = jnp.zeros((1, 8, HD), F32)

    loads[4].wait()
    loads[5].wait()
    for a in range(2):
        for h in range(HEADS):
            for t in range(SLOTS // CHUNK):
                rows = slice(t * CHUNK, (t + 1) * CHUNK)
                kvt[h, (1 - a) * HD : (2 - a) * HD, rows] = kv[a, rows, h * HD : (h + 1) * HD].T
    loads[2].wait()
    loads[3].wait()

    partner = (q, ctx_of(x, zl, 1 - k))

    def pass_on(slot):
        return pltpu.make_async_remote_copy(
            src_ref=gat.at[k, slot],
            dst_ref=gat.at[k, slot],
            send_sem=dsend.at[slot],
            recv_sem=drecv.at[slot],
            device_id=partner,
            device_id_type=MESH,
        )

    def from_partner(slot):
        return pltpu.make_async_remote_copy(
            src_ref=gat.at[1 - k, slot],
            dst_ref=gat.at[1 - k, slot],
            send_sem=dsend.at[slot],
            recv_sem=drecv.at[slot],
            device_id=partner,
            device_id_type=MESH,
        )

    def arrived(slot):
        return pltpu.make_async_remote_copy(
            src_ref=gat.at[k, slot],
            dst_ref=gat.at[k, slot],
            send_sem=bsend.at[0],
            recv_sem=brecv.at[slot],
            device_id=partner,
            device_id_type=MESH,
        )

    def heads_of(a, h, lo, n):
        return gat[a, lo : lo + n, :, h * HD : (h + 1) * HD].reshape(n * 32, HD)

    kept = {}

    def forward(half, h):
        lanes = slice(half * HD, (half + 1) * HD)
        cols = slice(h * HD, (h + 1) * HD)
        queries = heads_of(0, h, half * 4, 4)
        peak = jnp.full((1, HD), DEAD, F32)
        for t in range(SLOTS // CHUNK):
            rows = slice(t * CHUNK, (t + 1) * CHUNK)
            score = dot_nt(kv[0, rows, cols], queries) * SCALE + bias[h, rows, :]
            w32[h, rows, lanes] = score
            peak = jnp.maximum(peak, jnp.max(score, axis=0, keepdims=True))
        total = jnp.zeros((1, HD), F32)
        for t in range(SLOTS // CHUNK):
            rows = slice(t * CHUNK, (t + 1) * CHUNK)
            weight = jnp.exp(w32[h, rows, lanes] - peak)
            w32[h, rows, lanes] = weight
            w16[h, rows, lanes] = weight.astype(BF16)
            total = total + jnp.sum(weight, axis=0, keepdims=True)
        inverse = 1.0 / total
        mixed = dot(kvt[h], w16[h, :, lanes]) * inverse
        grads = heads_of(1, h, half * 4, 4).T.astype(F32)
        mean = jnp.sum(mixed[0:HD] * grads, axis=0, keepdims=True)
        mx[h : h + 1, lanes] = peak
        sx[half, pl.ds(g, 1), h : h + 1, :] = (peak + jnp.log(total)).reshape(1, 1, HD)
        sx[half, pl.ds(g, 1), 4 + h : 5 + h, :] = mean.reshape(1, 1, HD)
        kept[half, h] = (mixed.astype(BF16), mean, inverse)

    def stats_copy(half, gp, device, out):
        slot = g if out else gp
        return pltpu.make_async_remote_copy(
            src_ref=sx.at[half, slot], dst_ref=sx.at[half, slot],
            send_sem=xsend.at[half, gp], recv_sem=xrecv.at[half, slot],
            device_id=device, device_id_type=MESH,
        )

    stat_sends = []

    def send_stats(half):
        for dg in range(1, 8):
            gp, device = xk_peer(dg)
            copy = stats_copy(half, gp, device, True)
            copy.start()
            stat_sends.append(copy)

    def shares_copy(half, h, gp, device, out):
        return pltpu.make_async_remote_copy(
            src_ref=sf.at[half, h, gp], dst_ref=rx.at[half, h, g if out else gp],
            send_sem=fsend.at[half, h, gp], recv_sem=frecv.at[half, h, g if out else gp],
            device_id=device, device_id_type=MESH,
        )

    def shares(half, h):
        lanes = slice(half * HD, (half + 1) * HD)
        cols = slice(h * HD, (h + 1) * HD)
        mixed, mean, inverse = kept[half, h]
        grads = heads_of(1, h, half * 4, 4)
        for t in range(SLOTS // CHUNK):
            rows = slice(t * CHUNK, (t + 1) * CHUNK)
            dprob = dot_nt(kv[1, rows, cols], grads)
            dp[h, rows, lanes] = dprob
            dsb[h, rows, lanes] = (w32[h, rows, lanes] * (dprob - mean)).astype(BF16)
        slope = (dot(kvt[h, HD : 2 * HD, :], dsb[h, :, lanes]) * inverse).astype(BF16)
        turned = jnp.concatenate([mixed, slope], axis=0)
        rows = dot_nt(perm[...].astype(BF16), turned).astype(BF16)
        sf[half, h] = rows.reshape(8, 16, 3 * HD)
        for dg in range(1, 8):
            gp, device = xk_peer(dg)
            copy = shares_copy(half, h, gp, device, True)
            copy.start()
            stat_sends.append(copy)

    passed = []
    for half in range(2):
        slots = [lax.rem(y + d, 4) for d in (1, 3, 2)] if half == 0 else [4, 5, 6, 7]
        for slot in slots:
            arrived(slot).wait_recv()
            copy = pass_on(slot)
            copy.start()
            passed.append(copy)
        for slot in slots:
            from_partner(slot).wait_recv()
        for h in range(HEADS):
            forward(half, h)
        send_stats(half)
        for h in range(HEADS):
            shares(half, h)

    def merge(parts):
        logs, means = parts[:, 0:4, :], parts[:, 4:8, :]
        top = jnp.max(logs, axis=0)
        share = jnp.exp(logs - top[None])
        whole = jnp.sum(share, axis=0)
        return top + jnp.log(whole), jnp.sum(share * means, axis=0) / whole

    for half in range(2):
        for dg in range(1, 8):
            gp, device = xk_peer(dg)
            stats_copy(half, gp, device, False).wait_recv()
        logs, means = merge(sx[half])
        sz[half, pl.ds(zl, 1), 0:4, :] = logs[None]
        sz[half, pl.ds(zl, 1), 4:8, :] = means[None]

    def merged_copy(half, zp, out):
        slot = zl if out else zp
        return pltpu.make_async_remote_copy(
            src_ref=sz.at[half, slot], dst_ref=sz.at[half, slot],
            send_sem=zsend.at[half, zp], recv_sem=zrecv.at[half, slot],
            device_id=(q, ctx_of(x, zp, k)), device_id_type=MESH,
        )

    for half in range(2):
        for d in range(1, 4):
            copy = merged_copy(half, lax.rem(zl + d, 4), True)
            copy.start()
            stat_sends.append(copy)
    final_stats = []
    columns = []
    for half in range(2):
        for d in range(1, 4):
            merged_copy(half, lax.rem(zl + d, 4), False).wait_recv()
        log_total, delta = merge(sz[half])
        final_stats.append((log_total, delta))
        gain = jnp.exp(sx[half, :, 0:4, :] - log_total[None])
        tilt = gain * (sx[half, :, 4:8, :] - delta[None])
        both = jnp.concatenate([gain, tilt], axis=1).reshape(64, HD)
        columns.append(
            lax.dot_general(
                pick, both, NT, preferred_element_type=F32, precision=lax.Precision.HIGHEST
            )
        )

    for half in range(2):
        for h in range(HEADS):
            rx[half, h, pl.ds(g, 1)] = sf[half, h, pl.ds(g, 1)]
            for dg in range(1, 8):
                gp, device = xk_peer(dg)
                shares_copy(half, h, gp, device, False).wait_recv()
            attn_rows = jnp.zeros((16, HD), F32)
            grad_rows = jnp.zeros((16, HD), F32)
            for s in range(8):
                gain = columns[half][:, s * 8 + h : s * 8 + h + 1]
                tilt = columns[half][:, s * 8 + 4 + h : s * 8 + 5 + h]
                part = rx[half, h, s].astype(F32)
                attn_rows = attn_rows + gain * part[:, 0:HD]
                grad_rows = grad_rows + (tilt * part[:, HD : 2 * HD] + gain * part[:, 2 * HD :])
            fb[pl.ds(half * HD + h, 16, stride=8), :] = attn_rows
            fb[pl.ds(half * HD + HEADS + h, 16, stride=8), :] = grad_rows * SCALE
    sy[...] = fb[...].astype(BF16).reshape(32, 8, HD)

    me = zl * 8 + q

    def row_copy(rel, dz, dy, out):
        zp, yp, hp = lax.rem(zl + dz, 4), lax.rem(y + dy, 4), lax.rem(zh + rel, 2)
        e = rel * 16 + zp * 4 + yp
        qp = yp * 2 + hp
        other = zp * 8 + qp
        return pltpu.make_async_remote_copy(
            src_ref=sy.at[e], dst_ref=ry.at[me] if out else ry.at[other],
            send_sem=ysend.at[e], recv_sem=yrecv.at[me] if out else yrecv.at[other],
            device_id=(qp, ctx_of(x, zp, k)), device_id_type=MESH,
        )

    steps = [
        (rel, dz, dy)
        for rel in (1, 0) for dz in (2, 1, 3, 0) for dy in (2, 1, 3, 0)
        if rel or dz or dy
    ]
    for step in steps:
        copy = row_copy(*step, True)
        copy.start()
        stat_sends.append(copy)
    ry[pl.ds(me, 1)] = sy[pl.ds(zl * 4 + y, 1)]

    for h in range(HEADS):
        cols = slice(h * HD, (h + 1) * HD)
        factor = jnp.concatenate(
            [jnp.exp(mx[h : h + 1, half * HD : (half + 1) * HD] - final_stats[half][0][h : h + 1])
             for half in range(2)], axis=1)
        delta = jnp.concatenate([final_stats[half][1][h : h + 1] for half in range(2)], axis=1)
        for t in range(SLOTS // HD):
            rows = slice(t * HD, (t + 1) * HD)
            prob = w32[h, rows, :] * factor
            pb[h, rows, :] = prob.astype(BF16)
            dsb[h, rows, :] = (prob * (dp[h, rows, :] - delta)).astype(BF16)
        for t in range(SLOTS // CHUNK):
            rows = slice(t * CHUNK, (t + 1) * CHUNK)
            kg_ref[rows, cols] = (dot(dsb[h, rows, :], heads_of(0, h, 0, 8)) * SCALE).astype(BF16)
            vg_ref[rows, cols] = dot(pb[h, rows, :], heads_of(1, h, 0, 8)).astype(BF16)

    for step in steps:
        row_copy(*step, False).wait_recv()
    final = jnp.sum(ry[...].astype(F32).reshape(4, 8, 8, HD), axis=0)
    for qd in range(8):
        for h in range(HEADS):
            cols = slice((qd * HEADS + h) * HD, (qd * HEADS + h + 1) * HD)
            attn_ref[:, cols] = final[qd, h : h + 1, :].astype(BF16)
            dq_ref[:, cols] = final[qd, HEADS + h : HEADS + h + 1, :].astype(BF16)

    for copy in sends + passed + stat_sends:
        copy.wait_send()

    @pl.when(edge)
    def _():
        for copy in cross:
            copy.wait_send()


def write_out(attn_in, dq_in, kg_in, vg_in, attn_out, dq_out, kg_out, vg_out, sems):
    pairs = ((kg_in, kg_out), (vg_in, vg_out), (attn_in, attn_out), (dq_in, dq_out))
    copies = [pltpu.make_async_copy(a, b, sems.at[n]) for n, (a, b) in enumerate(pairs)]
    for copy in copies:
        copy.start()
    for copy in copies:
        copy.wait()


def local(query_states, key_states, value_states, level_ids, level_bias, live_counts, out_grad):
    hbm = pl.BlockSpec(memory_space=pltpu.HBM)
    vmem = pl.BlockSpec(memory_space=pltpu.VMEM)
    dma = pltpu.SemaphoreType.DMA
    arrays = (
        query_states, key_states, value_states, level_ids, level_bias, live_counts, out_grad
    )
    shapes = ((1, 3072), (1, 3072), key_states.shape, value_states.shape)
    results = pl.pallas_call(
        kernel,
        name="framepack",
        out_shape=tuple(pltpu.VMEM(shape, BF16) for shape in shapes),
        in_specs=[hbm] * 7,
        out_specs=(vmem,) * 4,
        scratch_shapes=[
            pltpu.VMEM((2, 32, 3072), BF16),
            pltpu.VMEM((2, 8, 32, COLS), BF16),
            pltpu.VMEM((2, SLOTS, COLS), BF16),
            pltpu.VMEM((HEADS, 2 * HD, SLOTS), BF16),
            pltpu.VMEM((HEADS, SLOTS, HD), F32),
            pltpu.VMEM((HD, HD), F32),
            pltpu.VMEM((HEADS, SLOTS, ROWS), F32),
            pltpu.VMEM((HEADS, SLOTS, ROWS), BF16),
            pltpu.VMEM((HEADS, SLOTS, ROWS), F32),
            pltpu.VMEM((HEADS, SLOTS, ROWS), BF16),
            pltpu.VMEM((HEADS, SLOTS, ROWS), BF16),
            pltpu.VMEM((8, ROWS), F32),
            pltpu.VMEM((2, 8, 8, HD), F32),
            pltpu.VMEM((2, 4, 8, HD), F32),
            pltpu.VMEM((2, HEADS, 8, 16, COLS), BF16),
            pltpu.VMEM((2, HEADS, 8, 16, COLS), BF16),
            pltpu.VMEM((ROWS, HD), F32),
            pltpu.VMEM((32, 8, HD), BF16),
            pltpu.VMEM((32, 8, HD), BF16),
            pltpu.SMEM((SLOTS,), jnp.int32),
            pltpu.SMEM((5, 24), F32),
            pltpu.SMEM((1,), jnp.int32),
            dma((9,)),
            dma((12,)), dma((8,)),
            dma((8,)), dma((8,)),
            dma((2, 8)), dma((2, 8)),
            dma((2, 4)), dma((2, 4)),
            dma((2, HEADS, 8)), dma((2, HEADS, 8)),
            dma((32,)), dma((32,)),
        ],
        compiler_params=pltpu.CompilerParams(
            collective_id=0, has_side_effects=True, vmem_limit_bytes=32 * 1024 * 1024
        ),
    )(*(a if a is live_counts else pltpu.with_memory_space_constraint(a, pltpu.HBM) for a in arrays))
    return pl.pallas_call(
        write_out,
        name="write_out",
        out_shape=tuple(jax.ShapeDtypeStruct(shape, BF16) for shape in shapes),
        in_specs=[vmem] * 4,
        out_specs=(hbm,) * 4,
        scratch_shapes=[dma((4,))],
    )(*(pltpu.with_memory_space_constraint(a, pltpu.VMEM) for a in results))


def solution(mesh):
    placed = (
        P("query", None),
        P("ctx", "query"),
        P("ctx", "query"),
        P("ctx"),
        P(),
        P("ctx"),
        P("query", None),
    )
    return jax.shard_map(
        local,
        mesh=mesh,
        in_specs=placed,
        out_specs=(
            P(("query", "ctx"), None),
            P(("query", "ctx"), None),
            P("ctx", "query"),
            P("ctx", "query"),
        ),
        check_vma=False,
    )
```

time: 46.7 us -> 40.2 us (0.86)
  local copies, waits for them, and re-layouts: 4.97 us -> 0 us
  Pallas kernels: 40.3 us -> 38.8 us
    unnamed x8 -> x0, local copies, waits for them, and re-layouts: 4.97 us -> none
    pallas_call x1 -> x2, Pallas kernels: 40.3 us -> 38.8 us  [the longest x1 37.6 us: local(): pl.pallas_call(kernel, name='framepack', out_shape=tuple((pltpu.VMEM(shap...]
where the time goes in v2:
time: 40.2 us; the launch traced here: 40.1 us
  Pallas kernels  38.8 us (97%)
  between operations  1.29 us (3%)
    pallas_call x1, Pallas kernels, local(): pl.pallas_call(kernel, name='framepack', out_shape=tuple((pltpu.VMEM(shap...  37.6 us
    pallas_call x1, Pallas kernels, local(): pl.pallas_call(write_out, name='write_out', out_shape=tuple((jax.ShapeDty...  1.18 us

profile of v2, /device:TPU:1, one launch (start us, length us, event | category | flops | bytes accessed | tf_op | source)
XLA Modules:
  0.0 40.1 jit_solution(12756784901427176936)
XLA Ops:
  1.3 37.6 %framepack.1 = (bf16[1,3072]{1,0:T(2,128)(2,1)S(1)}, bf16[1,3072]{1,0:T(2,128)(2,1)S(1)}, bf16[1024,384]{1,0:T(8,128)(2,1)S(1)}, bf16[1024,384]{1,0:T(8,128)(2,1)S(1)}) custom-call(bf16[32,3072]{1,0:T(8,128)(2,1)} %q_hbm.1, bf16[1024,384]{1,0:T(8,128)(2,1)} %k_hbm.1, bf16[1024,384]{1,0:T(8,128)(2,1)} %v_hbm.1, s32[1024]{0:T(1024)} %lid_hbm.1, ...), custom_call_target="tpu_custom_call" | custom-call | tf_op jit(solution)/shard_map/framepack/pallas_call | solution.py:423
  38.9 1.2 %write_out.1 = (bf16[1,3072]{1,0:T(2,128)(2,1)}, bf16[1,3072]{1,0:T(2,128)(2,1)}, bf16[1024,384]{1,0:T(8,128)(2,1)}, bf16[1024,384]{1,0:T(8,128)(2,1)}) custom-call(bf16[1,3072]{1,0:T(2,128)(2,1)S(1)} %get-tuple-element.8.attn_in, bf16[1,3072]{1,0:T(2,128)(2,1)S(1)} %get-tuple-element.9.dq_in, bf16[1024,384]{1,0:T(8,128)(2,1)S(1)} %get-tuple-element.10.kg_in, ...), custom_call_target="tpu_custom_call" | custom-call | tf_op jit(solution)/shard_map/write_out/pallas_call | solution.py:464

commit v3 on v0

v3 whole, which is shorter than its diff:
```python
import math

import jax
import jax.numpy as jnp
from jax import lax
from jax.experimental import pallas as pl
from jax.experimental.pallas import tpu as pltpu
from jax.sharding import PartitionSpec as P

MESH = pl.DeviceIdType.MESH
F32 = jnp.float32
BF16 = jnp.bfloat16
HD = 128
HEADS = 3
COLS = HEADS * HD
ROWS = 128
SLOTS = 1024
BOTH = 2 * SLOTS
RUNS = SLOTS // 16
CHUNK = 256
SCALE = 1.0 / math.sqrt(HD)
NT = (((1,), (1,)), ((), ()))
DEAD = -1e30


def dot_nt(a, b):
    return lax.dot_general(a, b, NT, preferred_element_type=F32)


def dot(a, b):
    return jnp.dot(a, b, preferred_element_type=F32)


def kernel(
    q_hbm, k_hbm, v_hbm, lid_hbm, lb_hbm, lc_hbm, g_hbm,
    attn_ref, dq_ref, kg_ref, vg_ref,
    own, gat, kv, kvt, table, bias, perm, w32, w16, dp, pb, dsb, mx,
    sx, sz, sf, rx, fb, sy, ry, kvo, xs, xr, lid, lb, lc,
    ld, dsend, drecv, bsend, brecv, xsend, xrecv, zsend, zrecv,
    fsend, frecv, ysend, yrecv, gsend, grecv,
):
    q = lax.axis_index("query")
    c = lax.axis_index("ctx")
    y, zh = q // 2, q % 2
    x, zl, k = c // 8, (c // 2) % 4, c % 2
    first, second = k == 0, k == 1

    def ctx_of(xx, zz, kk):
        return xx * 8 + zz * 2 + kk

    def load(src, dst, n):
        copy = pltpu.make_async_copy(src, dst, ld.at[n])
        copy.start()
        return copy

    loads = [
        load(q_hbm, own.at[0], 0),
        load(g_hbm, own.at[1], 1),
        load(lid_hbm, lid, 2),
        load(lb_hbm, lb, 3),
        load(lc_hbm, lc, 4),
        load(k_hbm, kv.at[0, 0:SLOTS], 5),
        load(v_hbm, kv.at[1, 0:SLOTS], 6),
    ]

    edge = zl % 3 == 0
    near, far = 3 - zl, 2 - zl // 3
    source = jnp.where(zl < 2, 3, 0)
    partner = (q, ctx_of(x, zl, 1 - k))
    ys = [lax.rem(y + d, 4) for d in range(4)]
    xs_of = [lax.rem(x + d, 4) for d in range(4)]
    zs = [lax.rem(zl + d, 4) for d in range(4)]
    barrier = pltpu.get_barrier_semaphore()

    def greet(device):
        pl.semaphore_signal(barrier, inc=1, device_id=device, device_id_type=MESH)

    for d in range(1, 4):
        greet((q, ctx_of(xs_of[d], zl, k)))
        greet((q, ctx_of(x, zs[d], k)))
    greet(partner)

    @pl.when(first)
    def _():
        for d in range(4):
            greet((ys[d] * 2 + 1 - zh, ctx_of(x, source, 1)))
        for d in range(1, 4):
            greet((ys[d] * 2 + zh, c))
        pl.semaphore_wait(barrier, 10)

    @pl.when(jnp.logical_and(second, edge))
    def _():
        for d in range(4):
            greet((ys[d] * 2 + 1 - zh, ctx_of(x, far, 1)))
            greet((ys[d] * 2 + 1 - zh, ctx_of(x, near, 1)))
        pl.semaphore_wait(barrier, 23)

    @pl.when(jnp.logical_and(second, jnp.logical_not(edge)))
    def _():
        for d in range(4):
            greet((ys[d] * 2 + 1 - zh, ctx_of(x, source, 1)))
        pl.semaphore_wait(barrier, 11)

    loads[0].wait()
    loads[1].wait()

    def remote(src, dst, send, recv, device):
        return pltpu.make_async_remote_copy(
            src_ref=src, dst_ref=dst, send_sem=send, recv_sem=recv,
            device_id=device, device_id_type=MESH,
        )

    def block_send(h, yd, half, zz):
        qd = yd * 2 + half
        cols = pl.ds(pl.multiple_of(qd * COLS + h * HD, HD), HD)
        remote(
            own.at[:, :, cols], gat.at[h, :, y], bsend.at[0], brecv.at[h],
            (qd, ctx_of(x, zz, k)),
        ).start()

    @pl.when(first)
    def _():
        for h in range(HEADS):
            for d in (2, 1, 3):
                block_send(h, ys[d], zh, zl)
            cols = pl.ds(pl.multiple_of(q * COLS + h * HD, HD), HD)
            gat[h, :, pl.ds(y, 1)] = own[:, :, cols].reshape(2, 1, 32, HD)

    @pl.when(jnp.logical_and(second, edge))
    def _():
        for h in range(HEADS):
            for d in (2, 1, 3, 0):
                block_send(h, ys[d], 1 - zh, far)
                block_send(h, ys[d], 1 - zh, near)

    loads[2].wait()
    loads[3].wait()
    loads[4].wait()

    def fill(t, carry):
        level = lid[t * 16]
        for h in range(HEADS):
            table[0, pl.ds(h * RUNS + t, 1), :] = jnp.full((1, HD), lb[level, q * HEADS + h], F32)
        return carry

    lax.fori_loop(0, RUNS, fill, 0)
    table[0, HEADS * RUNS :, :] = jnp.full((8, HD), lc[0].astype(F32), F32)
    loads[5].wait()
    loads[6].wait()
    swaps = [
        remote(table.at[0], table.at[1], dsend.at[0], drecv.at[0], partner),
        remote(kv.at[0, 0:SLOTS], kv.at[0, SLOTS:BOTH], dsend.at[1], drecv.at[1], partner),
        remote(kv.at[1, 0:SLOTS], kv.at[1, SLOTS:BOTH], dsend.at[2], drecv.at[2], partner),
    ]
    for copy in swaps:
        copy.start()

    p_id = lax.broadcasted_iota(jnp.int32, (HD, HD), 0)
    i_id = lax.broadcasted_iota(jnp.int32, (HD, HD), 1)
    perm[...] = jnp.where(i_id == ((p_id & 3) << 5) + (p_id >> 2), 1.0, 0.0)
    fb[...] = jnp.zeros_like(fb)
    sx[pl.ds(x, 1)] = jnp.zeros((1, 8, HD), F32)

    def prepare(part):
        def spread(t, carry):
            slot = lax.broadcasted_iota(jnp.int32, (16, HD), 0) + t * 16
            alive = slot.astype(F32) < table[part, HEADS * RUNS : HEADS * RUNS + 1, :]
            at = pl.ds(pl.multiple_of(part * SLOTS + t * 16, 16), 16)
            for h in range(HEADS):
                bias[h, at, :] = jnp.where(alive, table[part, pl.ds(h * RUNS + t, 1), :], DEAD)
            return carry

        lax.fori_loop(0, RUNS, spread, 0, unroll=4)
        for a in range(2):
            for h in range(HEADS):
                for t in range(SLOTS // CHUNK):
                    rows = slice(part * SLOTS + t * CHUNK, part * SLOTS + (t + 1) * CHUNK)
                    kvt[h, (1 - a) * HD : (2 - a) * HD, rows] = kv[a, rows, h * HD : (h + 1) * HD].T

    prepare(0)
    for copy in swaps:
        copy.wait_recv()
    prepare(1)

    chunks = [slice(t * CHUNK, (t + 1) * CHUNK) for t in range(BOTH // CHUNK)]

    def rows_of(a, h):
        return gat[h, a].reshape(ROWS, HD)

    def forward(h):
        cols = slice(h * HD, (h + 1) * HD)
        queries = rows_of(0, h)
        peak = jnp.full((1, HD), DEAD, F32)
        for rows in chunks:
            score = dot_nt(kv[0, rows, cols], queries) * SCALE + bias[h, rows, :]
            w32[h, rows, :] = score
            peak = jnp.maximum(peak, jnp.max(score, axis=0, keepdims=True))
        total = jnp.zeros((1, HD), F32)
        for rows in chunks:
            weight = jnp.exp(w32[h, rows, :] - peak)
            w32[h, rows, :] = weight
            w16[h, rows, :] = weight.astype(BF16)
            total = total + jnp.sum(weight, axis=0, keepdims=True)
        inverse = 1.0 / total
        mixed = dot(kvt[h], w16[h]) * inverse
        grads = rows_of(1, h).T.astype(F32)
        mean = jnp.sum(mixed[0:HD] * grads, axis=0, keepdims=True)
        mx[h : h + 1, :] = peak
        sx[pl.ds(x, 1), h : h + 1, :] = (peak + jnp.log(total)).reshape(1, 1, HD)
        sx[pl.ds(x, 1), 4 + h : 5 + h, :] = mean.reshape(1, 1, HD)
        return mixed.astype(BF16), mean, inverse

    def shares(h, kept):
        cols = slice(h * HD, (h + 1) * HD)
        mixed, mean, inverse = kept
        grads = rows_of(1, h)
        for rows in chunks:
            dprob = dot_nt(kv[1, rows, cols], grads)
            dp[h, rows, :] = dprob
            dsb[h, rows, :] = (w32[h, rows, :] * (dprob - mean)).astype(BF16)
        slope = (dot(kvt[h, HD : 2 * HD, :], dsb[h]) * inverse).astype(BF16)
        turned = jnp.concatenate([mixed, slope], axis=0)
        sf[h] = dot_nt(perm[...].astype(BF16), turned).astype(BF16).reshape(4, 32, COLS)
        for d in (2, 1, 3):
            remote(
                sf.at[h, xs_of[d]], rx.at[h, x], fsend.at[0], frecv.at[h],
                (q, ctx_of(xs_of[d], zl, k)),
            ).start()

    def await_recv(ref, sem):
        remote(ref, ref, sem, sem, partner).wait_recv()

    def await_send(ref, sem):
        remote(ref, ref, sem, sem, partner).wait_send()

    for h in range(HEADS):
        @pl.when(first)
        def _():
            await_recv(gat.at[h, :, 0:3], brecv.at[h])

        @pl.when(second)
        def _():
            await_recv(gat.at[h], brecv.at[h])

        kept = forward(h)
        if h == HEADS - 1:
            for d in (2, 1, 3):
                remote(
                    sx.at[x], sx.at[x], xsend.at[0], xrecv.at[0], (q, ctx_of(xs_of[d], zl, k))
                ).start()
        shares(h, kept)

    def merge(parts):
        logs, means = parts[:, 0:4, :], parts[:, 4:8, :]
        top = jnp.max(logs, axis=0)
        share = jnp.exp(logs - top[None])
        whole = jnp.sum(share, axis=0)
        return top + jnp.log(whole), jnp.sum(share * means, axis=0) / whole

    await_recv(sx.at[0:3], xrecv.at[0])
    logs, means = merge(sx[...])
    sz[pl.ds(zl, 1), 0:4, :] = logs[None]
    sz[pl.ds(zl, 1), 4:8, :] = means[None]
    for d in (2, 1, 3):
        remote(
            sz.at[zl], sz.at[zl], zsend.at[0], zrecv.at[0], (q, ctx_of(x, zs[d], k))
        ).start()
    own_rows = lax.broadcasted_iota(jnp.int32, (32, HD), 0) + x * 32
    own_lane = ((own_rows & 3) << 5) + (own_rows >> 2)
    pick = jnp.where(lax.broadcasted_iota(jnp.int32, (32, HD), 1) == own_lane, 1.0, 0.0)
    await_recv(sz.at[0:3], zrecv.at[0])
    log_total, delta = merge(sz[...])
    gain = jnp.exp(sx[:, 0:4, :] - log_total[None])
    tilt = gain * (sx[:, 4:8, :] - delta[None])
    both = jnp.concatenate([gain, tilt], axis=1).reshape(32, HD)
    columns = lax.dot_general(
        pick, both, NT, preferred_element_type=F32, precision=lax.Precision.HIGHEST
    )

    for h in range(HEADS):
        rx[h, pl.ds(x, 1)] = sf[h, pl.ds(x, 1)]
        await_recv(rx.at[h, 0:3], frecv.at[h])
        attn_rows = jnp.zeros((32, HD), F32)
        grad_rows = jnp.zeros((32, HD), F32)
        for s in range(4):
            gain_s = columns[:, s * 8 + h : s * 8 + h + 1]
            tilt_s = columns[:, s * 8 + 4 + h : s * 8 + 5 + h]
            part = rx[h, s].astype(F32)
            attn_rows = attn_rows + gain_s * part[:, 0:HD]
            grad_rows = grad_rows + (tilt_s * part[:, HD : 2 * HD] + gain_s * part[:, 2 * HD :])
        fb[pl.ds(h, 32, stride=8), :] = attn_rows
        fb[pl.ds(HEADS + h, 32, stride=8), :] = grad_rows * SCALE
    sy[...] = fb[...].astype(BF16).reshape(32, 8, HD)

    me = zl * 8 + q

    def row_send(dz, dy, dk):
        kp = lax.rem(k + dk, 2)
        remote(
            sy.at[zs[dz] * 8 + kp * 4 + ys[dy]], ry.at[me], ysend.at[0], yrecv.at[0],
            (ys[dy] * 2 + lax.rem(zh + k, 2), ctx_of(x, zs[dz], kp)),
        ).start()

    for dz in (2, 1, 3, 0):
        for dy in (2, 1, 3, 0):
            for dk in (1, 0):
                if dz or dy or dk:
                    row_send(dz, dy, dk)

    @pl.when(second)
    def _():
        row_send(0, 0, 0)

    @pl.when(first)
    def _():
        ry[pl.ds(me, 1)] = sy[pl.ds(zl * 8 + y, 1)]

    for h in range(HEADS):
        cols = slice(h * HD, (h + 1) * HD)
        factor = jnp.exp(mx[h : h + 1, :] - log_total[h : h + 1])
        center = delta[h : h + 1]
        for rows in chunks[::-1]:
            prob = w32[h, rows, :] * factor
            pb[h, rows, :] = prob.astype(BF16)
            dsb[h, rows, :] = (prob * (dp[h, rows, :] - center)).astype(BF16)
        half = len(chunks) // 2
        for n, rows in enumerate(chunks[half:]):
            xs[h, 0, chunks[n], :] = (dot(dsb[h, rows, :], rows_of(0, h)) * SCALE).astype(BF16)
            xs[h, 1, chunks[n], :] = dot(pb[h, rows, :], rows_of(1, h)).astype(BF16)
        remote(xs.at[h], xr.at[h], gsend.at[0], grecv.at[h], partner).start()
        for rows in chunks[:half]:
            kvo[0, rows, cols] = dot(dsb[h, rows, :], rows_of(0, h)) * SCALE
            kvo[1, rows, cols] = dot(pb[h, rows, :], rows_of(1, h))
    for h in range(HEADS):
        cols = slice(h * HD, (h + 1) * HD)
        await_recv(xr.at[h], grecv.at[h])
        kg_ref[:, cols] = (kvo[0, :, cols] + xr[h, 0].astype(F32)).astype(BF16)
        vg_ref[:, cols] = (kvo[1, :, cols] + xr[h, 1].astype(F32)).astype(BF16)

    @pl.when(first)
    def _():
        await_recv(ry.at[0:31], yrecv.at[0])

    @pl.when(second)
    def _():
        await_recv(ry, yrecv.at[0])

    final = jnp.sum(ry[...].astype(F32).reshape(4, 8, 8, HD), axis=0)
    for qd in range(8):
        for h in range(HEADS):
            cols = slice((qd * HEADS + h) * HD, (qd * HEADS + h + 1) * HD)
            attn_ref[:, cols] = final[qd, h : h + 1, :].astype(BF16)
            dq_ref[:, cols] = final[qd, HEADS + h : HEADS + h + 1, :].astype(BF16)

    for copy in swaps:
        copy.wait_send()
    await_send(sx.at[0:3], xsend.at[0])
    await_send(sz.at[0:3], zsend.at[0])
    await_send(sf.at[:, 0:3], fsend.at[0])
    await_send(xs, gsend.at[0])

    @pl.when(first)
    def _():
        await_send(gat.at[:, :, 0:3], bsend.at[0])
        await_send(sy.at[0:31], ysend.at[0])

    @pl.when(second)
    def _():
        await_send(sy, ysend.at[0])

    @pl.when(jnp.logical_and(second, edge))
    def _():
        await_send(own, bsend.at[0])


def write_out(attn_in, dq_in, kg_in, vg_in, attn_out, dq_out, kg_out, vg_out, sems):
    pairs = ((kg_in, kg_out), (vg_in, vg_out), (attn_in, attn_out), (dq_in, dq_out))
    copies = [pltpu.make_async_copy(a, b, sems.at[n]) for n, (a, b) in enumerate(pairs)]
    for copy in copies:
        copy.start()
    for copy in copies:
        copy.wait()


def local(query_states, key_states, value_states, level_ids, level_bias, live_counts, out_grad):
    hbm = pl.BlockSpec(memory_space=pltpu.HBM)
    vmem = pl.BlockSpec(memory_space=pltpu.VMEM)
    dma = pltpu.SemaphoreType.DMA
    arrays = (
        query_states, key_states, value_states, level_ids, level_bias, live_counts, out_grad
    )
    shapes = ((1, 3072), (1, 3072), key_states.shape, value_states.shape)
    results = pl.pallas_call(
        kernel,
        name="framepack",
        out_shape=tuple(pltpu.VMEM(shape, BF16) for shape in shapes),
        in_specs=[hbm] * 7,
        out_specs=(vmem,) * 4,
        scratch_shapes=[
            pltpu.VMEM((2, 32, 3072), BF16),
            pltpu.VMEM((HEADS, 2, 4, 32, HD), BF16),
            pltpu.VMEM((2, BOTH, COLS), BF16),
            pltpu.VMEM((HEADS, 2 * HD, BOTH), BF16),
            pltpu.VMEM((2, HEADS * RUNS + 8, HD), F32),
            pltpu.VMEM((HEADS, BOTH, HD), F32),
            pltpu.VMEM((HD, HD), F32),
            pltpu.VMEM((HEADS, BOTH, ROWS), F32),
            pltpu.VMEM((HEADS, BOTH, ROWS), BF16),
            pltpu.VMEM((HEADS, BOTH, ROWS), F32),
            pltpu.VMEM((HEADS, BOTH, ROWS), BF16),
            pltpu.VMEM((HEADS, BOTH, ROWS), BF16),
            pltpu.VMEM((8, ROWS), F32),
            pltpu.VMEM((4, 8, HD), F32),
            pltpu.VMEM((4, 8, HD), F32),
            pltpu.VMEM((HEADS, 4, 32, COLS), BF16),
            pltpu.VMEM((HEADS, 4, 32, COLS), BF16),
            pltpu.VMEM((32 * 8, HD), F32),
            pltpu.VMEM((32, 8, HD), BF16),
            pltpu.VMEM((32, 8, HD), BF16),
            pltpu.VMEM((2, SLOTS, COLS), F32),
            pltpu.VMEM((HEADS, 2, SLOTS, HD), BF16),
            pltpu.VMEM((HEADS, 2, SLOTS, HD), BF16),
            pltpu.SMEM((SLOTS,), jnp.int32),
            pltpu.SMEM((5, 24), F32),
            pltpu.SMEM((1,), jnp.int32),
            dma((7,)),
            dma((3,)), dma((3,)),
            dma((1,)), dma((HEADS,)),
            dma((1,)), dma((1,)),
            dma((1,)), dma((1,)),
            dma((1,)), dma((HEADS,)),
            dma((1,)), dma((1,)),
            dma((1,)), dma((HEADS,)),
        ],
        compiler_params=pltpu.CompilerParams(
            collective_id=0, has_side_effects=True, vmem_limit_bytes=40 * 1024 * 1024
        ),
    )(*(a if a is live_counts else pltpu.with_memory_space_constraint(a, pltpu.HBM) for a in arrays))
    return pl.pallas_call(
        write_out,
        name="write_out",
        out_shape=tuple(jax.ShapeDtypeStruct(shape, BF16) for shape in shapes),
        in_specs=[vmem] * 4,
        out_specs=(hbm,) * 4,
        scratch_shapes=[dma((4,))],
    )(*(pltpu.with_memory_space_constraint(a, pltpu.VMEM) for a in results))


def solution(mesh):
    placed = (
        P("query", None),
        P("ctx", "query"),
        P("ctx", "query"),
        P("ctx"),
        P(),
        P("ctx"),
        P("query", None),
    )
    return jax.shard_map(
        local,
        mesh=mesh,
        in_specs=placed,
        out_specs=(
            P(("query", "ctx"), None),
            P(("query", "ctx"), None),
            P("ctx", "query"),
            P("ctx", "query"),
        ),
        check_vma=False,
    )
```

time: 185 us -> 34.7 us (0.19)
  starting transfers between devices: 45.6 us -> 0 us
  waiting for transfers between devices: 40 us -> 0 us
  blocking collectives: 39.9 us -> 0 us
  Pallas kernels: 0 us -> 33.3 us
  local copies, waits for them, and re-layouts: 29.4 us -> 0 us
  matrix products: 17.8 us -> 0 us
  other arithmetic: 9.17 us -> 0 us
    all_to_all x8 -> x0, starting transfers between devices: 45.6 us -> none  [the longest x3 14.8 us: sum_at_owner(): pieces = lax.all_to_all(split_up(x, dim, peers), axis, 0, 0, tiled=True)]
    all_to_all x8 -> x0, waiting for transfers between devices: 40 us -> none  [the longest x3 14.4 us: sum_at_owner(): pieces = lax.all_to_all(split_up(x, dim, peers), axis, 0, 0, tiled=True)]
    all_gather x1 -> x0, blocking collectives: 39.9 us -> none  [gather_turned(): out = lax.all_gather(both, axis, axis=0, tiled=True)]
    pallas_call x0 -> x2, Pallas kernels: none -> 33.3 us  [the longest x1 32.2 us: local(): pl.pallas_call(kernel, name='framepack', out_shape=tuple((pltpu.VMEM(shap...]
    dot_general x7 -> x0, matrix products: 17.8 us -> none  [the longest x1 6.05 us: local(): jnp.einsum('hcbrk,cbrhd->bkhd', dscores.reshape(block_shape), queries.res...]
    unnamed x28 -> x0, local copies, waits for them, and re-layouts: 12 us -> none
    another operation x4 -> x0, local copies, waits for them, and re-layouts: 5.4 us -> none  [the longest x2 3.34 us: local(): grad_heads = grads_in.reshape(query_count, head_count, head_size)]
    all_to_all x4 -> x0, local copies, waits for them, and re-layouts: 4.97 us -> none  [the longest x2 3.27 us: local(): lax.all_to_all(out_grad, 'query', split_axis=1, concat_axis=0, tiled=True)]
  transfers between devices with their start and end apart: 8 -> 0, of which waited for: 8 -> 0; matrix products, arithmetic and copies ran while one was open for 23% -> 0% of each run, Pallas kernels for 0% -> 0%
where the time goes in v3:
time: 34.7 us; the launch traced here: 34.6 us
  Pallas kernels  33.3 us (96%)
  between operations  1.29 us (4%)
    pallas_call x1, Pallas kernels, local(): pl.pallas_call(kernel, name='framepack', out_shape=tuple((pltpu.VMEM(shap...  32.2 us
    pallas_call x1, Pallas kernels, local(): pl.pallas_call(write_out, name='write_out', out_shape=tuple((jax.ShapeDty...  1.18 us

profile of v3, /device:TPU:1, one launch (start us, length us, event | category | flops | bytes accessed | tf_op | source)
XLA Modules:
  0.0 34.6 jit_solution(3143722448834305722)
XLA Ops:
  1.3 32.2 %framepack.1 = (bf16[1,3072]{1,0:T(2,128)(2,1)S(1)}, bf16[1,3072]{1,0:T(2,128)(2,1)S(1)}, bf16[1024,384]{1,0:T(8,128)(2,1)S(1)}, bf16[1024,384]{1,0:T(8,128)(2,1)S(1)}) custom-call(bf16[32,3072]{1,0:T(8,128)(2,1)} %q_hbm.1, bf16[1024,384]{1,0:T(8,128)(2,1)} %k_hbm.1, bf16[1024,384]{1,0:T(8,128)(2,1)} %v_hbm.1, s32[1024]{0:T(1024)} %lid_hbm.1, ...), custom_call_target="tpu_custom_call" | custom-call | tf_op jit(solution)/shard_map/framepack/pallas_call | solution.py:393
  33.4 1.2 %write_out.1 = (bf16[1,3072]{1,0:T(2,128)(2,1)}, bf16[1,3072]{1,0:T(2,128)(2,1)}, bf16[1024,384]{1,0:T(8,128)(2,1)}, bf16[1024,384]{1,0:T(8,128)(2,1)}) custom-call(bf16[1,3072]{1,0:T(2,128)(2,1)S(1)} %get-tuple-element.8.attn_in, bf16[1,3072]{1,0:T(2,128)(2,1)S(1)} %get-tuple-element.9.dq_in, bf16[1024,384]{1,0:T(8,128)(2,1)S(1)} %get-tuple-element.10.kg_in, ...), custom_call_target="tpu_custom_call" | custom-call | tf_op jit(solution)/shard_map/write_out/pallas_call | solution.py:439

commit v4 on v3

--- a/solution.py
+++ b/solution.py
@@ -35,8 +35,8 @@
     q_hbm, k_hbm, v_hbm, lid_hbm, lb_hbm, lc_hbm, g_hbm,
     attn_ref, dq_ref, kg_ref, vg_ref,
     own, gat, kv, kvt, table, bias, perm, w32, w16, dp, pb, dsb, mx,
-    sx, sz, sf, rx, fb, sy, ry, kvo, xs, xr, lid, lb, lc,
-    ld, dsend, drecv, bsend, brecv, xsend, xrecv, zsend, zrecv,
+    sx, sf, rx, fb, sy, ry, kvo, xs, xr, lid, lb, lc,
+    ld, dsend, drecv, bsend, brecv, xsend, xrecv, token,
     fsend, frecv, ysend, yrecv, gsend, grecv,
 ):
     q = lax.axis_index("query")
@@ -65,7 +65,6 @@
 
     edge = zl % 3 == 0
     near, far = 3 - zl, 2 - zl // 3
-    source = jnp.where(zl < 2, 3, 0)
     partner = (q, ctx_of(x, zl, 1 - k))
     ys = [lax.rem(y + d, 4) for d in range(4)]
     xs_of = [lax.rem(x + d, 4) for d in range(4)]
@@ -76,30 +75,34 @@
         pl.semaphore_signal(barrier, inc=1, device_id=device, device_id_type=MESH)
 
     for d in range(1, 4):
+        greet((q, ctx_of(x, zs[d], 0)))
+        greet((q, ctx_of(x, zs[d], 1)))
         greet((q, ctx_of(xs_of[d], zl, k)))
-        greet((q, ctx_of(x, zs[d], k)))
     greet(partner)
 
     @pl.when(first)
     def _():
-        for d in range(4):
-            greet((ys[d] * 2 + 1 - zh, ctx_of(x, source, 1)))
         for d in range(1, 4):
             greet((ys[d] * 2 + zh, c))
-        pl.semaphore_wait(barrier, 10)
+        pl.semaphore_wait(barrier, 13)
 
     @pl.when(jnp.logical_and(second, edge))
     def _():
         for d in range(4):
+            greet((ys[d] * 2 + 1 - zh, ctx_of(x, near, 1)))
             greet((ys[d] * 2 + 1 - zh, ctx_of(x, far, 1)))
-            greet((ys[d] * 2 + 1 - zh, ctx_of(x, near, 1)))
-        pl.semaphore_wait(barrier, 23)
+        pl.semaphore_wait(barrier, 18)
 
     @pl.when(jnp.logical_and(second, jnp.logical_not(edge)))
     def _():
         for d in range(4):
-            greet((ys[d] * 2 + 1 - zh, ctx_of(x, source, 1)))
-        pl.semaphore_wait(barrier, 11)
+            greet((ys[d] * 2 + 1 - zh, ctx_of(x, jnp.where(zl < 2, 3, 0), 1)))
+        pl.semaphore_wait(barrier, 14)
+
+    for d in range(1, 4):
+        pl.semaphore_signal(
+            token, inc=1, device_id=(q, ctx_of(xs_of[d], zl, k)), device_id_type=MESH
+        )
 
     loads[0].wait()
     loads[1].wait()
@@ -114,7 +117,7 @@
         qd = yd * 2 + half
         cols = pl.ds(pl.multiple_of(qd * COLS + h * HD, HD), HD)
         remote(
-            own.at[:, :, cols], gat.at[h, :, y], bsend.at[0], brecv.at[h],
+            own.at[:, :, cols], gat.at[h, :, y], bsend.at[0], brecv.at[h, y],
             (qd, ctx_of(x, zz, k)),
         ).start()
 
@@ -159,7 +162,8 @@
     i_id = lax.broadcasted_iota(jnp.int32, (HD, HD), 1)
     perm[...] = jnp.where(i_id == ((p_id & 3) << 5) + (p_id >> 2), 1.0, 0.0)
     fb[...] = jnp.zeros_like(fb)
-    sx[pl.ds(x, 1)] = jnp.zeros((1, 8, HD), F32)
+    here = zl * 4 + x
+    sx[pl.ds(here, 1)] = jnp.zeros((1, 8, HD), F32)
 
     def prepare(part):
         def spread(t, carry):
@@ -206,8 +210,8 @@
         grads = rows_of(1, h).T.astype(F32)
         mean = jnp.sum(mixed[0:HD] * grads, axis=0, keepdims=True)
         mx[h : h + 1, :] = peak
-        sx[pl.ds(x, 1), h : h + 1, :] = (peak + jnp.log(total)).reshape(1, 1, HD)
-        sx[pl.ds(x, 1), 4 + h : 5 + h, :] = mean.reshape(1, 1, HD)
+        sx[pl.ds(here, 1), h : h + 1, :] = (peak + jnp.log(total)).reshape(1, 1, HD)
+        sx[pl.ds(here, 1), 4 + h : 5 + h, :] = mean.reshape(1, 1, HD)
         return mixed.astype(BF16), mean, inverse
 
     def shares(h, kept):
@@ -233,22 +237,30 @@
     def await_send(ref, sem):
         remote(ref, ref, sem, sem, partner).wait_send()
 
+    kept = []
     for h in range(HEADS):
         @pl.when(first)
         def _():
-            await_recv(gat.at[h, :, 0:3], brecv.at[h])
+            for d in (1, 3, 2):
+                await_recv(gat.at[h, :, ys[d]], brecv.at[h, ys[d]])
 
         @pl.when(second)
         def _():
-            await_recv(gat.at[h], brecv.at[h])
-
-        kept = forward(h)
-        if h == HEADS - 1:
-            for d in (2, 1, 3):
+            for d in (2, 3, 1, 0):
+                await_recv(gat.at[h, :, ys[d]], brecv.at[h, ys[d]])
+
+        kept.append(forward(h))
+        if h < 2:
+            shares(h, kept[h])
+    pl.semaphore_wait(token, 3)
+    for dz in (2, 1, 3, 0):
+        for dx in (2, 1, 3, 0):
+            if dz or dx:
                 remote(
-                    sx.at[x], sx.at[x], xsend.at[0], xrecv.at[0], (q, ctx_of(xs_of[d], zl, k))
+                    sx.at[here], sx.at[here], xsend.at[0], xrecv.at[0],
+                    (q, ctx_of(xs_of[dx], zs[dz], k)),
                 ).start()
-        shares(h, kept)
+    shares(2, kept[2])
 
     def merge(parts):
         logs, means = parts[:, 0:4, :], parts[:, 4:8, :]
@@ -257,29 +269,25 @@
         whole = jnp.sum(share, axis=0)
         return top + jnp.log(whole), jnp.sum(share * means, axis=0) / whole
 
-    await_recv(sx.at[0:3], xrecv.at[0])
-    logs, means = merge(sx[...])
-    sz[pl.ds(zl, 1), 0:4, :] = logs[None]
-    sz[pl.ds(zl, 1), 4:8, :] = means[None]
-    for d in (2, 1, 3):
-        remote(
-            sz.at[zl], sz.at[zl], zsend.at[0], zrecv.at[0], (q, ctx_of(x, zs[d], k))
-        ).start()
     own_rows = lax.broadcasted_iota(jnp.int32, (32, HD), 0) + x * 32
     own_lane = ((own_rows & 3) << 5) + (own_rows >> 2)
     pick = jnp.where(lax.broadcasted_iota(jnp.int32, (32, HD), 1) == own_lane, 1.0, 0.0)
-    await_recv(sz.at[0:3], zrecv.at[0])
-    log_total, delta = merge(sz[...])
-    gain = jnp.exp(sx[:, 0:4, :] - log_total[None])
-    tilt = gain * (sx[:, 4:8, :] - delta[None])
-    both = jnp.concatenate([gain, tilt], axis=1).reshape(32, HD)
-    columns = lax.dot_general(
-        pick, both, NT, preferred_element_type=F32, precision=lax.Precision.HIGHEST
-    )
+
+    def columns_of(gain, tilt, n):
+        both = jnp.concatenate([gain, tilt], axis=-2).reshape(n * 8, HD)
+        return lax.dot_general(
+            pick, both, NT, preferred_element_type=F32, precision=lax.Precision.HIGHEST
+        )
 
     for h in range(HEADS):
         rx[h, pl.ds(x, 1)] = sf[h, pl.ds(x, 1)]
         await_recv(rx.at[h, 0:3], frecv.at[h])
+    await_recv(sx.at[0:15], xrecv.at[0])
+    log_total, delta = merge(sx[...])
+    row = sx[pl.ds(zl * 4, 4)]
+    gain = jnp.exp(row[:, 0:4, :] - log_total[None])
+    columns = columns_of(gain, gain * (row[:, 4:8, :] - delta[None]), 4)
+    for h in range(HEADS):
         attn_rows = jnp.zeros((32, HD), F32)
         grad_rows = jnp.zeros((32, HD), F32)
         for s in range(4):
@@ -301,15 +309,15 @@
             (ys[dy] * 2 + lax.rem(zh + k, 2), ctx_of(x, zs[dz], kp)),
         ).start()
 
-    for dz in (2, 1, 3, 0):
-        for dy in (2, 1, 3, 0):
+    for dy in (2, 1, 3, 0):
+        for dz in (0, 1, 3, 2):
             for dk in (1, 0):
                 if dz or dy or dk:
                     row_send(dz, dy, dk)
-
-    @pl.when(second)
-    def _():
-        row_send(0, 0, 0)
+        if dy == 1:
+            @pl.when(second)
+            def _():
+                row_send(0, 0, 0)
 
     @pl.when(first)
     def _():
@@ -354,8 +362,7 @@
 
     for copy in swaps:
         copy.wait_send()
-    await_send(sx.at[0:3], xsend.at[0])
-    await_send(sz.at[0:3], zsend.at[0])
+    await_send(sx.at[0:15], xsend.at[0])
     await_send(sf.at[:, 0:3], fsend.at[0])
     await_send(xs, gsend.at[0])
 
@@ -374,7 +381,10 @@
 
 
 def write_out(attn_in, dq_in, kg_in, vg_in, attn_out, dq_out, kg_out, vg_out, sems):
-    pairs = ((kg_in, kg_out), (vg_in, vg_out), (attn_in, attn_out), (dq_in, dq_out))
+    pairs = [(attn_in, attn_out), (dq_in, dq_out)]
+    for t in range(SLOTS // CHUNK):
+        rows = pl.ds(t * CHUNK, CHUNK)
+        pairs += [(kg_in.at[rows], kg_out.at[rows]), (vg_in.at[rows], vg_out.at[rows])]
     copies = [pltpu.make_async_copy(a, b, sems.at[n]) for n, (a, b) in enumerate(pairs)]
     for copy in copies:
         copy.start()
@@ -394,7 +404,7 @@
         kernel,
         name="framepack",
         out_shape=tuple(pltpu.VMEM(shape, BF16) for shape in shapes),
-        in_specs=[hbm] * 7,
+        in_specs=[hbm] * 5 + [pl.BlockSpec(memory_space=pl.ANY), hbm],
         out_specs=(vmem,) * 4,
         scratch_shapes=[
             pltpu.VMEM((2, 32, 3072), BF16),
@@ -410,8 +420,7 @@
             pltpu.VMEM((HEADS, BOTH, ROWS), BF16),
             pltpu.VMEM((HEADS, BOTH, ROWS), BF16),
             pltpu.VMEM((8, ROWS), F32),
-            pltpu.VMEM((4, 8, HD), F32),
-            pltpu.VMEM((4, 8, HD), F32),
+            pltpu.VMEM((16, 8, HD), F32),
             pltpu.VMEM((HEADS, 4, 32, COLS), BF16),
             pltpu.VMEM((HEADS, 4, 32, COLS), BF16),
             pltpu.VMEM((32 * 8, HD), F32),
@@ -425,9 +434,9 @@
             pltpu.SMEM((1,), jnp.int32),
             dma((7,)),
             dma((3,)), dma((3,)),
-            dma((1,)), dma((HEADS,)),
+            dma((1,)), dma((HEADS, 4)),
             dma((1,)), dma((1,)),
-            dma((1,)), dma((1,)),
+            pltpu.SemaphoreType.REGULAR,
             dma((1,)), dma((HEADS,)),
             dma((1,)), dma((1,)),
             dma((1,)), dma((HEADS,)),
@@ -442,7 +451,7 @@
         out_shape=tuple(jax.ShapeDtypeStruct(shape, BF16) for shape in shapes),
         in_specs=[vmem] * 4,
         out_specs=(hbm,) * 4,
-        scratch_shapes=[dma((4,))],
+        scratch_shapes=[dma((2 + 2 * (SLOTS // CHUNK),))],
     )(*(pltpu.with_memory_space_constraint(a, pltpu.VMEM) for a in results))
 
 

time: 34.7 us -> 32.4 us (0.934)
  Pallas kernels: 33.3 us -> 31 us
    pallas_call x1, Pallas kernels: 32.2 us -> 29.8 us  [local(): pl.pallas_call(kernel, name='framepack', out_shape=tuple((pltpu.VMEM(shap...]
where the time goes in v4:
time: 32.4 us; the launch traced here: 32.3 us
  Pallas kernels  31 us (96%)
  between operations  1.29 us (4%)
    pallas_call x1, Pallas kernels, local(): pl.pallas_call(kernel, name='framepack', out_shape=tuple((pltpu.VMEM(shap...  29.8 us
    pallas_call x1, Pallas kernels, local(): pl.pallas_call(write_out, name='write_out', out_shape=tuple((jax.ShapeDty...  1.23 us

profile of v4, /device:TPU:1, one launch (start us, length us, event | category | flops | bytes accessed | tf_op | source)
XLA Modules:
  0.0 32.3 jit_solution(15109975580947455521)
XLA Ops:
  1.3 29.8 %framepack.1 = (bf16[1,3072]{1,0:T(2,128)(2,1)S(1)}, bf16[1,3072]{1,0:T(2,128)(2,1)S(1)}, bf16[1024,384]{1,0:T(8,128)(2,1)S(1)}, bf16[1024,384]{1,0:T(8,128)(2,1)S(1)}) custom-call(bf16[32,3072]{1,0:T(8,128)(2,1)} %q_hbm.1, bf16[1024,384]{1,0:T(8,128)(2,1)} %k_hbm.1, bf16[1024,384]{1,0:T(8,128)(2,1)} %v_hbm.1, s32[1024]{0:T(1024)} %lid_hbm.1, ...), custom_call_target="tpu_custom_call" | custom-call | tf_op jit(solution)/shard_map/framepack/pallas_call | solution.py:403
  31.1 1.2 %write_out.1 = (bf16[1,3072]{1,0:T(2,128)(2,1)}, bf16[1,3072]{1,0:T(2,128)(2,1)}, bf16[1024,384]{1,0:T(8,128)(2,1)}, bf16[1024,384]{1,0:T(8,128)(2,1)}) custom-call(bf16[1,3072]{1,0:T(2,128)(2,1)S(1)} %get-tuple-element.8.attn_in, bf16[1,3072]{1,0:T(2,128)(2,1)S(1)} %get-tuple-element.9.dq_in, bf16[1024,384]{1,0:T(8,128)(2,1)S(1)} %get-tuple-element.10.kg_in, ...), custom_call_target="tpu_custom_call" | custom-call | tf_op jit(solution)/shard_map/write_out/pallas_call | solution.py:448

commit v5 on v4

--- a/solution.py
+++ b/solution.py
@@ -21,6 +21,7 @@
 SCALE = 1.0 / math.sqrt(HD)
 NT = (((1,), (1,)), ((), ()))
 DEAD = -1e30
+LOG2E = math.log2(math.e)
 
 
 def dot_nt(a, b):
@@ -34,7 +35,7 @@
 def kernel(
     q_hbm, k_hbm, v_hbm, lid_hbm, lb_hbm, lc_hbm, g_hbm,
     attn_ref, dq_ref, kg_ref, vg_ref,
-    own, gat, kv, kvt, table, bias, perm, w32, w16, dp, pb, dsb, mx,
+    own, gat, kv, kvt, table, bias, perm, work, w16, dp, pb, dsb, mx,
     sx, sf, rx, fb, sy, ry, kvo, xs, xr, lid, lb, lc,
     ld, dsend, drecv, bsend, brecv, xsend, xrecv, token,
     fsend, frecv, ysend, yrecv, gsend, grecv,
@@ -117,7 +118,7 @@
         qd = yd * 2 + half
         cols = pl.ds(pl.multiple_of(qd * COLS + h * HD, HD), HD)
         remote(
-            own.at[:, :, cols], gat.at[h, :, y], bsend.at[0], brecv.at[h, y],
+            own.at[:, :, cols], gat.at[h, :, y], bsend.at[0], brecv.at[h],
             (qd, ctx_of(x, zz, k)),
         ).start()
 
@@ -143,7 +144,9 @@
     def fill(t, carry):
         level = lid[t * 16]
         for h in range(HEADS):
-            table[0, pl.ds(h * RUNS + t, 1), :] = jnp.full((1, HD), lb[level, q * HEADS + h], F32)
+            table[0, pl.ds(h * RUNS + t, 1), :] = jnp.full(
+                (1, HD), lb[level, q * HEADS + h] * LOG2E, F32
+            )
         return carry
 
     lax.fori_loop(0, RUNS, fill, 0)
@@ -196,41 +199,45 @@
         queries = rows_of(0, h)
         peak = jnp.full((1, HD), DEAD, F32)
         for rows in chunks:
-            score = dot_nt(kv[0, rows, cols], queries) * SCALE + bias[h, rows, :]
-            w32[h, rows, :] = score
+            score = dot_nt(kv[0, rows, cols], queries) * (SCALE * LOG2E) + bias[h, rows, :]
+            work[rows, :] = score
             peak = jnp.maximum(peak, jnp.max(score, axis=0, keepdims=True))
         total = jnp.zeros((1, HD), F32)
         for rows in chunks:
-            weight = jnp.exp(w32[h, rows, :] - peak)
-            w32[h, rows, :] = weight
+            weight = jnp.exp2(work[rows, :] - peak)
             w16[h, rows, :] = weight.astype(BF16)
             total = total + jnp.sum(weight, axis=0, keepdims=True)
         inverse = 1.0 / total
         mixed = dot(kvt[h], w16[h]) * inverse
         grads = rows_of(1, h).T.astype(F32)
         mean = jnp.sum(mixed[0:HD] * grads, axis=0, keepdims=True)
+        peak = peak * (1.0 / LOG2E)
         mx[h : h + 1, :] = peak
         sx[pl.ds(here, 1), h : h + 1, :] = (peak + jnp.log(total)).reshape(1, 1, HD)
         sx[pl.ds(here, 1), 4 + h : 5 + h, :] = mean.reshape(1, 1, HD)
         return mixed.astype(BF16), mean, inverse
 
-    def shares(h, kept):
-        cols = slice(h * HD, (h + 1) * HD)
-        mixed, mean, inverse = kept
-        grads = rows_of(1, h)
-        for rows in chunks:
-            dprob = dot_nt(kv[1, rows, cols], grads)
-            dp[h, rows, :] = dprob
-            dsb[h, rows, :] = (w32[h, rows, :] * (dprob - mean)).astype(BF16)
-        slope = (dot(kvt[h, HD : 2 * HD, :], dsb[h]) * inverse).astype(BF16)
-        turned = jnp.concatenate([mixed, slope], axis=0)
-        sf[h] = dot_nt(perm[...].astype(BF16), turned).astype(BF16).reshape(4, 32, COLS)
+    def send_shares(h):
         for d in (2, 1, 3):
             remote(
                 sf.at[h, xs_of[d]], rx.at[h, x], fsend.at[0], frecv.at[h],
                 (q, ctx_of(xs_of[d], zl, k)),
             ).start()
 
+    def shares(h, kept):
+        cols = slice(h * HD, (h + 1) * HD)
+        mixed, mean, inverse = kept
+        turn = perm[...].astype(BF16)
+        grads = rows_of(1, h)
+        for rows in chunks:
+            dprob = dot_nt(kv[1, rows, cols], grads)
+            dp[h, rows, :] = dprob
+            dsb[h, rows, :] = (w16[h, rows, :].astype(F32) * (dprob - mean)).astype(BF16)
+        slope = (dot(kvt[h, HD : 2 * HD, :], dsb[h]) * inverse).astype(BF16)
+        turned = jnp.concatenate([mixed, slope], axis=0)
+        sf[h] = dot_nt(turn, turned).astype(BF16).reshape(4, 32, COLS)
+        send_shares(h)
+
     def await_recv(ref, sem):
         remote(ref, ref, sem, sem, partner).wait_recv()
 
@@ -241,20 +248,18 @@
     for h in range(HEADS):
         @pl.when(first)
         def _():
-            for d in (1, 3, 2):
-                await_recv(gat.at[h, :, ys[d]], brecv.at[h, ys[d]])
+            await_recv(gat.at[h, :, 0:3], brecv.at[h])
 
         @pl.when(second)
         def _():
-            for d in (2, 3, 1, 0):
-                await_recv(gat.at[h, :, ys[d]], brecv.at[h, ys[d]])
+            await_recv(gat.at[h], brecv.at[h])
 
         kept.append(forward(h))
         if h < 2:
             shares(h, kept[h])
     pl.semaphore_wait(token, 3)
-    for dz in (2, 1, 3, 0):
-        for dx in (2, 1, 3, 0):
+    for dx in (2, 1, 3, 0):
+        for dz in (2, 1, 3, 0):
             if dz or dx:
                 remote(
                     sx.at[here], sx.at[here], xsend.at[0], xrecv.at[0],
@@ -311,7 +316,7 @@
 
     for dy in (2, 1, 3, 0):
         for dz in (0, 1, 3, 2):
-            for dk in (1, 0):
+            for dk in (0, 1):
                 if dz or dy or dk:
                     row_send(dz, dy, dk)
         if dy == 1:
@@ -328,7 +333,7 @@
         factor = jnp.exp(mx[h : h + 1, :] - log_total[h : h + 1])
         center = delta[h : h + 1]
         for rows in chunks[::-1]:
-            prob = w32[h, rows, :] * factor
+            prob = w16[h, rows, :].astype(F32) * factor
             pb[h, rows, :] = prob.astype(BF16)
             dsb[h, rows, :] = (prob * (dp[h, rows, :] - center)).astype(BF16)
         half = len(chunks) // 2
@@ -381,10 +386,7 @@
 
 
 def write_out(attn_in, dq_in, kg_in, vg_in, attn_out, dq_out, kg_out, vg_out, sems):
-    pairs = [(attn_in, attn_out), (dq_in, dq_out)]
-    for t in range(SLOTS // CHUNK):
-        rows = pl.ds(t * CHUNK, CHUNK)
-        pairs += [(kg_in.at[rows], kg_out.at[rows]), (vg_in.at[rows], vg_out.at[rows])]
+    pairs = ((kg_in, kg_out), (vg_in, vg_out), (attn_in, attn_out), (dq_in, dq_out))
     copies = [pltpu.make_async_copy(a, b, sems.at[n]) for n, (a, b) in enumerate(pairs)]
     for copy in copies:
         copy.start()
@@ -414,7 +416,7 @@
             pltpu.VMEM((2, HEADS * RUNS + 8, HD), F32),
             pltpu.VMEM((HEADS, BOTH, HD), F32),
             pltpu.VMEM((HD, HD), F32),
-            pltpu.VMEM((HEADS, BOTH, ROWS), F32),
+            pltpu.VMEM((BOTH, ROWS), F32),
             pltpu.VMEM((HEADS, BOTH, ROWS), BF16),
             pltpu.VMEM((HEADS, BOTH, ROWS), F32),
             pltpu.VMEM((HEADS, BOTH, ROWS), BF16),
@@ -434,7 +436,7 @@
             pltpu.SMEM((1,), jnp.int32),
             dma((7,)),
             dma((3,)), dma((3,)),
-            dma((1,)), dma((HEADS, 4)),
+            dma((1,)), dma((HEADS,)),
             dma((1,)), dma((1,)),
             pltpu.SemaphoreType.REGULAR,
             dma((1,)), dma((HEADS,)),
@@ -451,7 +453,7 @@
         out_shape=tuple(jax.ShapeDtypeStruct(shape, BF16) for shape in shapes),
         in_specs=[vmem] * 4,
         out_specs=(hbm,) * 4,
-        scratch_shapes=[dma((2 + 2 * (SLOTS // CHUNK),))],
+        scratch_shapes=[dma((4,))],
     )(*(pltpu.with_memory_space_constraint(a, pltpu.VMEM) for a in results))
 
 

time: 32.4 us -> 31.9 us (0.985)
  Pallas kernels: 31 us -> 30.5 us
    pallas_call x1, Pallas kernels: 29.8 us -> 29.3 us  [local(): pl.pallas_call(kernel, name='framepack', out_shape=tuple((pltpu.VMEM(shap...]
where the time goes in v5:
time: 31.9 us; the launch traced here: 31.8 us
  Pallas kernels  30.5 us (96%)
  between operations  1.29 us (4%)
    pallas_call x1, Pallas kernels, local(): pl.pallas_call(kernel, name='framepack', out_shape=tuple((pltpu.VMEM(shap...  29.3 us
    pallas_call x1, Pallas kernels, local(): pl.pallas_call(write_out, name='write_out', out_shape=tuple((jax.ShapeDty...  1.18 us

profile of v5, /device:TPU:1, one launch (start us, length us, event | category | flops | bytes accessed | tf_op | source)
XLA Modules:
  0.0 31.8 jit_solution(6464039310304672226)
XLA Ops:
  1.3 29.3 %framepack.1 = (bf16[1,3072]{1,0:T(2,128)(2,1)S(1)}, bf16[1,3072]{1,0:T(2,128)(2,1)S(1)}, bf16[1024,384]{1,0:T(8,128)(2,1)S(1)}, bf16[1024,384]{1,0:T(8,128)(2,1)S(1)}) custom-call(bf16[32,3072]{1,0:T(8,128)(2,1)} %q_hbm.1, bf16[1024,384]{1,0:T(8,128)(2,1)} %k_hbm.1, bf16[1024,384]{1,0:T(8,128)(2,1)} %v_hbm.1, s32[1024]{0:T(1024)} %lid_hbm.1, ...), custom_call_target="tpu_custom_call" | custom-call | tf_op jit(solution)/shard_map/framepack/pallas_call | solution.py:405
  30.6 1.2 %write_out.1 = (bf16[1,3072]{1,0:T(2,128)(2,1)}, bf16[1,3072]{1,0:T(2,128)(2,1)}, bf16[1024,384]{1,0:T(8,128)(2,1)}, bf16[1024,384]{1,0:T(8,128)(2,1)}) custom-call(bf16[1,3072]{1,0:T(2,128)(2,1)S(1)} %get-tuple-element.8.attn_in, bf16[1,3072]{1,0:T(2,128)(2,1)S(1)} %get-tuple-element.9.dq_in, bf16[1024,384]{1,0:T(8,128)(2,1)S(1)} %get-tuple-element.10.kg_in, ...), custom_call_target="tpu_custom_call" | custom-call | tf_op jit(solution)/shard_map/write_out/pallas_call | solution.py:450

commit v6 on v5

--- a/solution.py
+++ b/solution.py
@@ -75,6 +75,17 @@
     def greet(device):
         pl.semaphore_signal(barrier, inc=1, device_id=device, device_id_type=MESH)
 
+    @pl.when(jnp.logical_and(second, edge))
+    def _():
+        for d in (2, 1, 3, 0):
+            greet((ys[d] * 2 + 1 - zh, ctx_of(x, far, 1)))
+            greet((ys[d] * 2 + 1 - zh, ctx_of(x, near, 1)))
+
+    @pl.when(jnp.logical_and(second, jnp.logical_not(edge)))
+    def _():
+        for d in (2, 1, 3, 0):
+            greet((ys[d] * 2 + 1 - zh, ctx_of(x, jnp.where(zl < 2, 3, 0), 1)))
+
     for d in range(1, 4):
         greet((q, ctx_of(x, zs[d], 0)))
         greet((q, ctx_of(x, zs[d], 1)))
@@ -87,18 +98,9 @@
             greet((ys[d] * 2 + zh, c))
         pl.semaphore_wait(barrier, 13)
 
-    @pl.when(jnp.logical_and(second, edge))
-    def _():
-        for d in range(4):
-            greet((ys[d] * 2 + 1 - zh, ctx_of(x, near, 1)))
-            greet((ys[d] * 2 + 1 - zh, ctx_of(x, far, 1)))
-        pl.semaphore_wait(barrier, 18)
-
-    @pl.when(jnp.logical_and(second, jnp.logical_not(edge)))
-    def _():
-        for d in range(4):
-            greet((ys[d] * 2 + 1 - zh, ctx_of(x, jnp.where(zl < 2, 3, 0), 1)))
-        pl.semaphore_wait(barrier, 14)
+    @pl.when(second)
+    def _():
+        pl.semaphore_wait(barrier, 14 + 4 * edge.astype(jnp.int32))
 
     for d in range(1, 4):
         pl.semaphore_signal(

time: 31.9 us -> 31.8 us (level)
  no operation moved by 1% of the time
where the time goes in v6:
time: 31.8 us; the launch traced here: 31.7 us
  Pallas kernels  30.4 us (96%)
  between operations  1.29 us (4%)
    pallas_call x1, Pallas kernels, local(): pl.pallas_call(kernel, name='framepack', out_shape=tuple((pltpu.VMEM(shap...  29.3 us
    pallas_call x1, Pallas kernels, local(): pl.pallas_call(write_out, name='write_out', out_shape=tuple((jax.ShapeDty...  1.18 us

profile of v6, /device:TPU:1, one launch (start us, length us, event | category | flops | bytes accessed | tf_op | source)
XLA Modules:
  0.0 31.7 jit_solution(3109484301863668853)
XLA Ops:
  1.3 29.3 %framepack.1 = (bf16[1,3072]{1,0:T(2,128)(2,1)S(1)}, bf16[1,3072]{1,0:T(2,128)(2,1)S(1)}, bf16[1024,384]{1,0:T(8,128)(2,1)S(1)}, bf16[1024,384]{1,0:T(8,128)(2,1)S(1)}) custom-call(bf16[32,3072]{1,0:T(8,128)(2,1)} %q_hbm.1, bf16[1024,384]{1,0:T(8,128)(2,1)} %k_hbm.1, bf16[1024,384]{1,0:T(8,128)(2,1)} %v_hbm.1, s32[1024]{0:T(1024)} %lid_hbm.1, ...), custom_call_target="tpu_custom_call" | custom-call | tf_op jit(solution)/shard_map/framepack/pallas_call | solution.py:407
  30.5 1.2 %write_out.1 = (bf16[1,3072]{1,0:T(2,128)(2,1)}, bf16[1,3072]{1,0:T(2,128)(2,1)}, bf16[1024,384]{1,0:T(8,128)(2,1)}, bf16[1024,384]{1,0:T(8,128)(2,1)}) custom-call(bf16[1,3072]{1,0:T(2,128)(2,1)S(1)} %get-tuple-element.8.attn_in, bf16[1,3072]{1,0:T(2,128)(2,1)S(1)} %get-tuple-element.9.dq_in, bf16[1024,384]{1,0:T(8,128)(2,1)S(1)} %get-tuple-element.10.kg_in, ...), custom_call_target="tpu_custom_call" | custom-call | tf_op jit(solution)/shard_map/write_out/pallas_call | solution.py:452
